TPU v7x, 32 devices: a whole 2x2x4 slice. The times are simulated.
32 devices in a mesh: rows: 32 (over z, y, x, core).
Axes of the slice: x: 2, y: 2, z: 4, core: 2. Of those that a mesh axis runs over, the one named last changes fastest.
Arguments:
- p_left: bfloat16 [120, 262144], P(None, 'rows'), may hold values from -0.5 to 0.5
- phi_right: bfloat16 [120, 262144], P(None, 'rows'), may hold values from -0.01171875 to 0.01171875
- v_cols: bfloat16 [40, 262144], P(None, 'rows'), may hold values from -6 to 6
- w_cols: bfloat16 [40, 262144], P(None, 'rows'), may hold values from -6 to 6
- residual: bfloat16 [262144], P('rows'), may hold values from -8 to 8, as said below
Outputs:
- update: float32 [262144], P('rows')
- q_left: bfloat16 [160, 262144], P(None, 'rows')
- q_right: bfloat16 [160, 262144], P(None, 'rows')
- rms_norms: float32 [2], replicated
Inputs may be any that keep to these rules, and one draw needn't show every extreme that they name: A residual that lies mostly in the span of the rows of v_cols.
All inputs are finite; a program needn't handle non-finite values.
Results may differ from a plain program's by a relative error of at most 0.0039.
Values may be sent and summed in bfloat16 or wider, within the bound.
No kernel may reach another device: no remote copies, remote signals or barrier semaphores. Data moves between devices by JAX's collectives and lax.ppermute only.
A program may use at most 128 MiB of HBM per device.

v0:
```python
import functools

import jax
import jax.numpy as jnp
from jax import lax
from jax.experimental import pallas as pl
from jax.experimental.pallas import tpu as pltpu
from jax.sharding import PartitionSpec as P

SINGLE = jnp.float32
HALF = jnp.bfloat16
LANES = 128
BLOCK = 8
HIGHEST = lax.Precision.HIGHEST
NT = (((1,), (1,)), ((), ()))
VMEM_LIMIT = 24 * 1024 * 1024
SORT_TILE = 256


def iota(shape, dim):
    return lax.broadcasted_iota(jnp.int32, shape, dim)


def dot_hi(a, b, dims=None):
    if dims is None:
        return jnp.dot(a, b, precision=HIGHEST, preferred_element_type=SINGLE)
    return lax.dot_general(a, b, dims, precision=HIGHEST, preferred_element_type=SINGLE)


def in_vmem(x):
    return pltpu.with_memory_space_constraint(x, pltpu.VMEM)


def in_hbm(*xs):
    return [pltpu.with_memory_space_constraint(x, pltpu.HBM) for x in xs]


def to_half(x):
    return x.astype(HALF).astype(SINGLE)


def sort_kernel(n, p_ref, w_ref, out_ref, turned):
    cross = out_ref.shape[1]
    wide = p_ref.shape[1]
    tile = SORT_TILE
    runs = tile // n
    row, column = iota((tile, tile), 0), iota((tile, tile), 1)
    wanted = lax.rem(row, runs) * n + lax.div(row, runs)
    permutation = jnp.where(column == wanted, 1.0, 0.0).astype(HALF)
    eye = jnp.where(iota((cross, cross), 0) == iota((cross, cross), 1), 1.0, 0.0).astype(HALF)
    pair = 16 // runs if runs < 16 else 1
    for at in range(0, wide, tile * pair):
        parts = []
        for i in range(pair):
            cut = slice(at + i * tile, at + (i + 1) * tile)
            both = jnp.concatenate([p_ref[:, cut].astype(SINGLE), w_ref[:, cut].astype(SINGLE)], 0)
            part = lax.dot_general(permutation, both.astype(HALF), NT, preferred_element_type=SINGLE)
            parts.append(part.reshape(n, runs, cross))
        rows = slice(at // n, at // n + runs * pair)
        turned[:, rows, :] = jnp.concatenate(parts, 1).astype(HALF)
    for owner in range(n):
        mine = lax.dot_general(eye, turned[owner], NT, preferred_element_type=SINGLE)
        out_ref[owner] = mine.astype(HALF)


def sort_by_owner(p_left, w_cols, n):
    rank, local = p_left.shape
    cols = w_cols.shape[0]
    share = local // n
    chunks = share // LANES if share % LANES == 0 else 1
    wide = local // chunks
    return pl.pallas_call(
        functools.partial(sort_kernel, n),
        grid=(chunks,),
        in_specs=[
            pl.BlockSpec((rank, wide), lambda i: (0, i)),
            pl.BlockSpec((cols, wide), lambda i: (0, i)),
        ],
        out_specs=pl.BlockSpec((n, rank + cols, share // chunks), lambda i: (0, 0, i)),
        out_shape=pltpu.HBM((n, rank + cols, share), HALF),
        scratch_shapes=[pltpu.VMEM((n, share // chunks, rank + cols), HALF)],
        compiler_params=pltpu.CompilerParams(vmem_limit_bytes=VMEM_LIMIT),
        name="sort_by_owner",
    )(*in_hbm(p_left, w_cols))


def gram_kernel(p_ref, w_ref, phi_ref, v_ref, res_ref, out_ref, left, right):
    at = pl.program_id(0)

    @pl.when(at == 0)
    def _():
        left[...] = jnp.zeros_like(left)
        right[...] = jnp.zeros_like(right)

    x = jnp.concatenate([p_ref[...].astype(SINGLE), w_ref[...].astype(SINGLE)], 0).astype(HALF)
    left[...] += lax.dot_general(x, x, NT, preferred_element_type=SINGLE)
    wide = res_ref.shape[1]
    last = jnp.where(iota((8, wide), 0) == 0, res_ref[...].astype(SINGLE), 0.0)
    y = jnp.concatenate([phi_ref[...].astype(SINGLE), v_ref[...].astype(SINGLE), last], 0).astype(HALF)
    right[...] += lax.dot_general(y, y, NT, preferred_element_type=SINGLE)

    @pl.when(at == pl.num_programs(0) - 1)
    def _():
        cross = left.shape[0]
        m = LANES
        e = cross - m
        rows, lanes = iota((m, m), 0), iota((m, m), 1)
        top_right = right[0:m, 0:m]
        out_ref[0:m, :] = jnp.where(lanes <= rows, left[0:m, 0:m], top_right)
        out_ref[m : m + e, :] = left[m:cross, 0:m]
        out_ref[m + e : m + 2 * e, :] = right[m:cross, 0:m]
        out_ref[m + 2 * e : m + 3 * e, :] = jnp.zeros((e, m), SINGLE)
        out_ref[m + 2 * e : m + 3 * e, 0:e] = left[m:cross, m:cross]
        out_ref[m + 2 * e : m + 3 * e, e : 2 * e] = right[m:cross, m:cross]
        base = m + 3 * e
        out_ref[base:, :] = jnp.zeros((out_ref.shape[0] - base, m), SINGLE)
        out_ref[base : base + 1, :] = jnp.sum(jnp.where(rows == lanes, top_right, 0.0), 0, keepdims=True)
        out_ref[base + 1 : base + 2, :] = right[cross : cross + 1, 0:m]
        out_ref[base + 2 : base + 3, 0 : e + 1] = right[cross : cross + 1, m : cross + 1]


def packed_rows(cross):
    used = LANES + 3 * (cross - LANES) + BLOCK
    return -(-used // (8 * BLOCK)) * 8 * BLOCK


def packed_grams(p_left, w_cols, phi_right, v_cols, residual):
    rank, local = p_left.shape
    cols = w_cols.shape[0]
    cross = rank + cols
    wide = min(local, 2048)
    spec = lambda rows: pl.BlockSpec((rows, wide), lambda i: (0, i))
    return pl.pallas_call(
        gram_kernel,
        grid=(local // wide,),
        in_specs=[spec(rank), spec(cols), spec(rank), spec(cols), spec(1)],
        out_specs=pl.BlockSpec((packed_rows(cross), LANES), lambda i: (0, 0)),
        out_shape=pltpu.VMEM((packed_rows(cross), LANES), SINGLE),
        scratch_shapes=[pltpu.VMEM((cross, cross), SINGLE), pltpu.VMEM((cross + 8, cross + 8), SINGLE)],
        compiler_params=pltpu.CompilerParams(vmem_limit_bytes=VMEM_LIMIT),
        name="packed_grams",
    )(*in_hbm(p_left, w_cols, phi_right, v_cols), residual.reshape(1, local))


def eliminate(refs, tops, k):
    panels = []
    for ref, top in zip(refs, tops):
        cross = ref.shape[1]
        x = ref[pl.ds(pl.multiple_of(k - top, BLOCK), BLOCK), :]
        lane, sub = iota((BLOCK, cross), 1), iota((BLOCK, cross), 0)
        column = [
            jnp.sum(jnp.where(lane == k + i, x, 0.0), 1, keepdims=True) for i in range(BLOCK)
        ]
        rel = lane - k
        x = jnp.where((rel >= 0) & (rel < BLOCK), jnp.where(rel == sub, 1.0, 0.0), x)
        panels.append([x, column, rel, sub])
    thin = iota((BLOCK, 1), 0)
    for i in range(BLOCK):
        for panel in panels:
            x, column, rel, sub = panel
            scale = lax.rsqrt(column[i][i : i + 1, :])
            factor = jnp.where(thin > i, column[i] * scale, 0.0)
            for j in range(i + 1, BLOCK):
                column[j] = column[j] - factor * (column[j][i : i + 1, :] * scale)
            row = x[i : i + 1, :] * scale
            panel[0] = jnp.where(sub == i, row, x - factor * row)
    for ref, top, (x, _, rel, _) in zip(refs, tops, panels):
        cross = ref.shape[1]
        right = jnp.where(rel >= BLOCK, x, 0.0)
        done = jnp.where(rel < BLOCK, x, 0.0)
        r0 = to_half(right)
        r1 = to_half(right - r0)
        r2 = right - r0 - r1
        x0 = to_half(x)
        x1 = to_half(x - x0)
        x2 = x - x0 - x1
        lhs = jnp.concatenate([r0, r0, r0, r1, r1, r2], 0)
        if top:
            lhs = jnp.concatenate([lhs, jnp.zeros((LANES - lhs.shape[0], cross), SINGLE)], 0)
            lhs = lhs.T[top:cross, 0 : 6 * BLOCK].astype(HALF)
        else:
            lhs = lhs.T.astype(HALF)
        rhs = jnp.concatenate([x0, x1, x2, x0, x1, x0], 0).astype(HALF)
        change = jnp.dot(lhs, rhs, preferred_element_type=SINGLE)
        here = iota(ref.shape, 1) - k
        ref[...] = jnp.where((here >= 0) & (here < BLOCK), 0.0, ref[...]) - change
        ref[pl.ds(pl.multiple_of(k - top, BLOCK), BLOCK), :] = done


def small_kernel(rank, count, g_ref, kl_ref, kr_ref, u_ref, rms_ref, left, right, tail):
    cross = left.shape[0]
    m = LANES
    e = cross - m
    base = m + 3 * e
    rows, lanes = iota((m, m), 0), iota((m, m), 1)
    top = g_ref[0:m, :]
    lower = jnp.where(lanes < rows, top, 0.0)
    upper = jnp.where(lanes > rows, top, 0.0)
    same = rows == lanes
    left[0:m, 0:m] = lower + lower.T + jnp.where(same, top, 0.0)
    right[0:m, 0:m] = upper + upper.T + jnp.where(same, g_ref[base : base + 1, :], 0.0)
    left[m:cross, 0:m] = g_ref[m : m + e, :]
    right[m:cross, 0:m] = g_ref[m + e : m + 2 * e, :]
    left[0:m, m:cross] = g_ref[m : m + e, :].T
    right[0:m, m:cross] = g_ref[m + e : m + 2 * e, :].T
    left[m:cross, m:cross] = g_ref[m + 2 * e : m + 3 * e, 0:e]
    right[m:cross, m:cross] = g_ref[m + 2 * e : m + 3 * e, e : 2 * e]
    g_left = left[...]
    g_right = right[...]
    res_first = g_ref[base + 1 : base + 2, :]
    res_rest = g_ref[base + 2 : base + 3, 0:e]
    res_row = jnp.concatenate([res_first, res_rest], 1)
    res_sq = g_ref[base + 2 : base + 3, e : e + 1]

    tail[...] = g_right[rank:cross, :]
    lax.fori_loop(
        rank // BLOCK, cross // BLOCK, lambda b, c: (eliminate([tail], [rank], b * BLOCK), c)[1], 0
    )
    low_lane = iota((cross - rank, cross), 1)
    low_row = iota((cross - rank, cross), 0)
    inverse = jnp.where(low_lane >= rank, tail[...], 0.0)
    eye = jnp.where(iota((rank, cross), 0) == iota((rank, cross), 1), 1.0, 0.0)

    mix = jnp.where(
        low_lane < rank, -to_half(g_right[rank:cross, :]), jnp.where(low_lane == low_row + rank, 1.0, 0.0)
    )
    to_tilde = jnp.concatenate([eye, mix], 0)
    t_right = jnp.concatenate([eye, inverse], 0)
    t_left = jnp.concatenate([eye, dot_hi(inverse, to_tilde)], 0)

    lane8 = iota((BLOCK, cross), 1)
    res8 = jnp.broadcast_to(res_row, (BLOCK, cross))
    half_way = dot_hi(jnp.where(lane8 >= rank, res8, 0.0), inverse, NT)
    coeffs = -dot_hi(half_way, inverse)
    u = dot_hi(jnp.where(lane8 < rank, -to_half(res8), coeffs), to_tilde)
    upd_sq = jnp.sum(dot_hi(u, g_left) * u, 1, keepdims=True)[0:1, :]
    u0 = to_half(u)
    u1 = to_half(u - u0)
    u2 = u - u0 - u1
    sub8 = iota((BLOCK, cross), 0)
    u_ref[...] = jnp.where(sub8 == 0, u0, jnp.where(sub8 == 1, u1, jnp.where(sub8 == 2, u2, 0.0)))
    lane_out = iota((1, LANES), 1)
    rms_ref[...] = jnp.sqrt(jnp.where(lane_out == 0, res_sq, upd_sq) / count)

    left[...] = dot_hi(dot_hi(t_left, g_left), t_left, NT)
    right[...] = dot_hi(dot_hi(t_right, g_right), t_right, NT)
    lax.fori_loop(
        0, cross // BLOCK, lambda b, c: (eliminate([left, right], [0, 0], b * BLOCK), c)[1], 0
    )
    for source, turn, out in ((left, t_left, kl_ref), (right, t_right, kr_ref)):
        k = dot_hi(source[...], turn)
        k0 = to_half(k)
        out[0:cross, :] = k0.astype(HALF)
        out[cross : 2 * cross, :] = (k - k0).astype(HALF)


def small_algebra(packed, rank, cols, count):
    cross = rank + cols
    vmem = pl.BlockSpec(memory_space=pltpu.VMEM)
    return pl.pallas_call(
        functools.partial(small_kernel, rank, count),
        in_specs=[vmem],
        out_specs=[vmem] * 4,
        out_shape=[
            pltpu.VMEM((2 * cross, cross), HALF),
            pltpu.VMEM((2 * cross, cross), HALF),
            pltpu.VMEM((BLOCK, cross), SINGLE),
            jax.ShapeDtypeStruct((1, LANES), SINGLE),
        ],
        scratch_shapes=[
            pltpu.VMEM((cross, cross), SINGLE),
            pltpu.VMEM((cross, cross), SINGLE),
            pltpu.VMEM((cols, cross), SINGLE),
        ],
        compiler_params=pltpu.CompilerParams(vmem_limit_bytes=VMEM_LIMIT),
        name="small_algebra",
    )(in_vmem(packed))


def right_kernel(p_ref, w_ref, phi_ref, v_ref, k_ref, u_ref, upd_ref, q_ref):
    cross = k_ref.shape[1]
    y = jnp.concatenate([phi_ref[...].astype(SINGLE), v_ref[...].astype(SINGLE)], 0).astype(HALF)
    both = jnp.dot(k_ref[...], y, preferred_element_type=SINGLE)
    q_ref[...] = (both[0:cross] + both[cross : 2 * cross]).astype(HALF)
    x = jnp.concatenate([p_ref[...].astype(SINGLE), w_ref[...].astype(SINGLE)], 0).astype(HALF)
    upd_ref[...] = jnp.sum(
        jnp.dot(u_ref[...].astype(HALF), x, preferred_element_type=SINGLE), 0, keepdims=True
    )


def right_products(p_left, w_cols, phi_right, v_cols, k_right, u):
    rank, local = p_left.shape
    cols = w_cols.shape[0]
    cross = rank + cols
    wide = min(local, 2048)
    spec = lambda rows: pl.BlockSpec((rows, wide), lambda i: (0, i))
    return pl.pallas_call(
        right_kernel,
        grid=(local // wide,),
        in_specs=[
            spec(rank), spec(cols), spec(rank), spec(cols),
            pl.BlockSpec((2 * cross, cross), lambda i: (0, 0)),
            pl.BlockSpec((BLOCK, cross), lambda i: (0, 0)),
        ],
        out_specs=[spec(1), spec(cross)],
        out_shape=[
            jax.ShapeDtypeStruct((1, local), SINGLE),
            jax.ShapeDtypeStruct((cross, local), HALF),
        ],
        compiler_params=pltpu.CompilerParams(vmem_limit_bytes=VMEM_LIMIT),
        name="right_products",
    )(*in_hbm(p_left, w_cols, phi_right, v_cols), in_vmem(k_right), in_vmem(u))


def left_kernel(x_ref, k_ref, q_ref):
    group, cross, share = x_ref.shape
    for i in range(group):
        both = jnp.dot(k_ref[...], x_ref[i], preferred_element_type=SINGLE)
        q_ref[:, i * share : (i + 1) * share] = (both[0:cross] + both[cross : 2 * cross]).astype(HALF)


def left_products(sorted_x, k_left):
    n, cross, share = sorted_x.shape
    group = max(1, 2048 // share)
    return pl.pallas_call(
        left_kernel,
        grid=(n // group,),
        in_specs=[
            pl.BlockSpec((group, cross, share), lambda i: (i, 0, 0)),
            pl.BlockSpec((2 * cross, cross), lambda i: (0, 0)),
        ],
        out_specs=pl.BlockSpec((cross, group * share), lambda i: (0, i)),
        out_shape=jax.ShapeDtypeStruct((cross, n * share), HALF),
        compiler_params=pltpu.CompilerParams(vmem_limit_bytes=VMEM_LIMIT),
        name="left_products",
    )(in_vmem(sorted_x), in_vmem(k_left))


def swap(x, reach):
    n = lax.axis_size("rows")
    return lax.ppermute(x, "rows", [(i, i ^ reach) for i in range(n)])


def sum_over_rest(x, reaches):
    me = lax.axis_index("rows")
    splits = []
    for reach in reaches:
        half = x.shape[0] // 2
        bit = lax.rem(lax.div(me, reach), 2)
        kept = lax.dynamic_slice_in_dim(x, bit * half, half)
        given = lax.dynamic_slice_in_dim(x, (1 - bit) * half, half)
        x = kept + swap(given, reach)
        splits.append((reach, bit))
    for reach, bit in reversed(splits):
        other = swap(x, reach)
        x = jnp.where(bit == 0, jnp.concatenate([x, other], 0), jnp.concatenate([other, x], 0))
    return x


def shards(p_left, phi_right, v_cols, w_cols, residual):
    rank, local = p_left.shape
    cols = v_cols.shape[0]
    n = lax.axis_size("rows")
    near = [1 << i for i in range(3)]
    far = [1 << i for i in range(3, n.bit_length() - 1)]
    packed = packed_grams(p_left, w_cols, phi_right, v_cols, residual)
    mine = sort_by_owner(p_left, w_cols, n)
    for reach in far[:-1]:
        packed = packed + swap(packed, reach)
    mine, packed = lax.optimization_barrier((mine, packed))
    other = swap(packed, far[-1])
    owned = lax.all_to_all(mine, "rows", split_axis=0, concat_axis=0, tiled=True)
    packed = packed + other
    packed = sum_over_rest(packed, near)
    k_left, k_right, u, rms = small_algebra(packed, rank, cols, float(local * n))
    update, q_right = right_products(p_left, w_cols, phi_right, v_cols, k_right, u)
    q_left = left_products(owned, k_left)
    return (update.reshape(local), q_left, q_right, rms[0, 0:2])


def solution(mesh):
    placed = (P(None, "rows"), P(None, "rows"), P(None, "rows"), P(None, "rows"), P("rows"))
    return jax.shard_map(
        shards,
        mesh=mesh,
        in_specs=placed,
        out_specs=(P("rows"), P(None, "rows"), P(None, "rows"), P()),
        check_vma=False,
    )
```

profile of v0, /device:TPU:0, one launch (start us, length us, event | category | flops | bytes accessed | tf_op | source)
XLA Modules:
  0.0 124.3 jit_solution(10824849300789722747)
XLA Ops:
  0.6 0.7 reshape.14.res_ref
  1.4 4.4 %packed_grams.1 = f32[256,128]{1,0:T(8,128)S(1)} custom-call(bf16[120,8192]{1,0:T(8,128)(2,1)} %p_ref.5, bf16[40,8192]{1,0:T(8,128)(2,1)} %w_ref.5, bf16[120,8192]{1,0:T(8,128)(2,1)} %phi_ref.3, bf16[40,8192]{1,0:T(8,128)(2,1)} %v_ref.3, bf16[1,8192]{1,0:T(2,128)(2,1)S(1)} %reshape.14.res_ref), custom_call_target="tpu_custom_call" | custom-call | tf_op jit(solution)/shard_map/packed_grams/pallas_call | solution.py:133
  5.8 3.1 %collective-permute-start = (f32[256,128]{1,0:T(8,128)S(1)}, f32[256,128]{1,0:T(8,128)S(1)}, u32[]{:S(2)}, u32[]{:S(2)}) collective-permute-start(f32[256,128]{1,0:T(8,128)S(1)} %packed_grams.1), channel_id=1, source_target_pairs={{0,8},{1,9},{2,10},{3,11},{4,12},{5,13},{6,14},{7,15},{8,0},{9,1},... | collective-permute-start | bytes 393224 | tf_op jit(solution)/shard_map/ppermute | solution.py:341
  8.9 5.3 %sort_by_owner.1 = bf16[32,160,256]{2,1,0:T(8,128)(2,1)} custom-call(bf16[120,8192]{1,0:T(8,128)(2,1)} %p_ref.5, bf16[40,8192]{1,0:T(8,128)(2,1)} %w_ref.5), custom_call_target="tpu_custom_call" | custom-call | tf_op jit(solution)/shard_map/sort_by_owner/pallas_call | solution.py:72
  14.2 0.0 collective-permute-done
  14.2 4.9 %all-to-all-start = ((bf16[32,160,256]{2,1,0:T(8,128)(2,1)}), bf16[32,160,256]{2,1,0:T(8,128)(2,1)S(1)}, u32[]{:S(2)}, u32[]{:S(2)}) async-start(bf16[32,160,256]{2,1,0:T(8,128)(2,1)} %sort_by_owner.1), calls=%async_computation | async-start | bytes 5242880 | tf_op jit(solution)/shard_map/all_to_all | solution.py:372
  19.1 2.7 %collective-permute-start.1 = (f32[256,128]{1,0:T(8,128)S(1)}, f32[256,128]{1,0:T(8,128)S(1)}, u32[]{:S(2)}, u32[]{:S(2)}) collective-permute-start(f32[256,128]{1,0:T(8,128)S(1)} %add.33), channel_id=1, source_target_pairs={{0,16},{1,17},{2,18},{3,19},{4,20},{5,21},{6,22},{7,23},{8,24},{9,... | collective-permute-start | bytes 393224 | tf_op jit(solution)/shard_map/ppermute | solution.py:341
  21.8 62.9 %collective-permute-done.1 = f32[256,128]{1,0:T(8,128)S(1)} collective-permute-done((f32[256,128]{1,0:T(8,128)S(1)}, f32[256,128]{1,0:T(8,128)S(1)}, u32[]{:S(2)}, u32[]{:S(2)}) %collective-permute-start.1) | collective-permute-done | bytes 131104 | tf_op jit(solution)/shard_map/ppermute | solution.py:341
  84.8 0.1 collective-permute-start.2
  84.9 1.2 collective-permute-done.2
  86.2 1.5 %collective-permute-start.3 = (f32[64,128]{1,0:T(8,128)S(1)}, f32[64,128]{1,0:T(8,128)S(1)}, u32[]{:S(2)}, u32[]{:S(2)}) collective-permute-start(f32[64,128]{1,0:T(8,128)S(1)} %constant_dynamic-slice_fusion.1), channel_id=1, source_target_pairs={{0,2},{1,3},{2,0},{3,1},{4,6},{5,7},{6,4},{7,5},{8,10},{9,11},{10,... | collective-permute-start | bytes 98312 | tf_op jit(solution)/shard_map/ppermute | solution.py:341
  87.7 2.5 %collective-permute-done.3 = f32[64,128]{1,0:T(8,128)S(1)} collective-permute-done((f32[64,128]{1,0:T(8,128)S(1)}, f32[64,128]{1,0:T(8,128)S(1)}, u32[]{:S(2)}, u32[]{:S(2)}) %collective-permute-start.3) | collective-permute-done | bytes 32800 | tf_op jit(solution)/shard_map/ppermute | solution.py:341
  90.2 1.4 %collective-permute-start.4 = (f32[32,128]{1,0:T(8,128)S(1)}, f32[32,128]{1,0:T(8,128)S(1)}, u32[]{:S(2)}, u32[]{:S(2)}) collective-permute-start(f32[32,128]{1,0:T(8,128)S(1)} %constant_dynamic-slice_fusion), channel_id=1, source_target_pairs={{0,4},{1,5},{2,6},{3,7},{4,0},{5,1},{6,2},{7,3},{8,12},{9,13},{10,... | collective-permute-start | bytes 49160 | tf_op jit(solution)/shard_map/ppermute | solution.py:341
  91.6 2.4 %collective-permute-done.4 = f32[32,128]{1,0:T(8,128)S(1)} collective-permute-done((f32[32,128]{1,0:T(8,128)S(1)}, f32[32,128]{1,0:T(8,128)S(1)}, u32[]{:S(2)}, u32[]{:S(2)}) %collective-permute-start.4) | collective-permute-done | bytes 16416 | tf_op jit(solution)/shard_map/ppermute | solution.py:341
  94.0 1.3 %collective-permute-start.5 = (f32[32,128]{1,0:T(8,128)S(1)}, f32[32,128]{1,0:T(8,128)S(1)}, u32[]{:S(2)}, u32[]{:S(2)}) collective-permute-start(f32[32,128]{1,0:T(8,128)S(1)} %dynamic-slice_add_fusion.2), channel_id=1, source_target_pairs={{0,4},{1,5},{2,6},{3,7},{4,0},{5,1},{6,2},{7,3},{8,12},{9,13},{10,... | collective-permute-start | bytes 49160 | tf_op jit(solution)/shard_map/ppermute | solution.py:341
  95.3 2.4 %collective-permute-done.5 = f32[32,128]{1,0:T(8,128)S(1)} collective-permute-done((f32[32,128]{1,0:T(8,128)S(1)}, f32[32,128]{1,0:T(8,128)S(1)}, u32[]{:S(2)}, u32[]{:S(2)}) %collective-permute-start.5) | collective-permute-done | bytes 16416 | tf_op jit(solution)/shard_map/ppermute | solution.py:341
  97.7 1.5 %collective-permute-start.6 = (f32[64,128]{1,0:T(8,128)S(1)}, f32[64,128]{1,0:T(8,128)S(1)}, u32[]{:S(2)}, u32[]{:S(2)}) collective-permute-start(f32[64,128]{1,0:T(8,128)S(1)} %maximum_select_fusion.2), channel_id=1, source_target_pairs={{0,2},{1,3},{2,0},{3,1},{4,6},{5,7},{6,4},{7,5},{8,10},{9,11},{10,... | collective-permute-start | bytes 98312 | tf_op jit(solution)/shard_map/ppermute | solution.py:341
  99.2 2.5 %collective-permute-done.6 = f32[64,128]{1,0:T(8,128)S(1)} collective-permute-done((f32[64,128]{1,0:T(8,128)S(1)}, f32[64,128]{1,0:T(8,128)S(1)}, u32[]{:S(2)}, u32[]{:S(2)}) %collective-permute-start.6) | collective-permute-done | bytes 32800 | tf_op jit(solution)/shard_map/ppermute | solution.py:341
  101.7 0.1 collective-permute-start.7
  101.7 1.2 collective-permute-done.7
  103.0 12.2 %small_algebra.1 = (bf16[320,160]{1,0:T(8,128)(2,1)S(1)}, bf16[320,160]{1,0:T(8,128)(2,1)S(1)}, f32[8,160]{1,0:T(8,128)S(1)}, f32[1,128]{1,0:T(1,128)S(1)}) custom-call(f32[256,128]{1,0:T(8,128)S(1)} %maximum_select_fusion.g_ref), custom_call_target="tpu_custom_call" | custom-call | tf_op jit(solution)/shard_map/small_algebra/pallas_call | solution.py:260
  115.2 5.5 %right_products.1 = (f32[1,8192]{1,0:T(1,128)}, bf16[160,8192]{1,0:T(8,128)(2,1)}) custom-call(bf16[120,8192]{1,0:T(8,128)(2,1)} %p_ref.5, bf16[40,8192]{1,0:T(8,128)(2,1)} %w_ref.5, bf16[120,8192]{1,0:T(8,128)(2,1)} %phi_ref.3, bf16[40,8192]{1,0:T(8,128)(2,1)} %v_ref.3, bf16[320,160]{1,0:T(8,128)(2,1)S(1)} %get-tuple-element.13.k_ref, ...), custom_call_target="tpu_custom_call" | custom-call | tf_op jit(solution)/shard_map/right_products/pallas_call | solution.py:297
  120.6 0.5 slice_bitcast_fusion
  121.2 0.0 all-to-all-done.x_ref
  121.2 3.2 %left_products.1 = bf16[160,8192]{1,0:T(8,128)(2,1)} custom-call(bf16[32,160,256]{2,1,0:T(8,128)(2,1)S(1)} %all-to-all-done.x_ref, bf16[320,160]{1,0:T(8,128)(2,1)S(1)} %get-tuple-element.17.k_ref), custom_call_target="tpu_custom_call" | custom-call | tf_op jit(solution)/shard_map/left_products/pallas_call | solution.py:325
  (11 shorter events, 0.1 us)
Async XLA Ops:
  5.8 8.4 %collective-permute-start = (f32[256,128]{1,0:T(8,128)S(1)}, f32[256,128]{1,0:T(8,128)S(1)}, u32[]{:S(2)}, u32[]{:S(2)}) collective-permute-start(f32[256,128]{1,0:T(8,128)S(1)} %packed_grams.1), channel_id=1, source_target_pairs={{0,8},{1,9},{2,10},{3,11},{4,12},{5,13},{6,14},{7,15},{8,0},{9,1},... | collective-permute-start | bytes 393224 | tf_op jit(solution)/shard_map/ppermute | solution.py:341
  14.2 106.9 %all-to-all-start = ((bf16[32,160,256]{2,1,0:T(8,128)(2,1)}), bf16[32,160,256]{2,1,0:T(8,128)(2,1)S(1)}, u32[]{:S(2)}, u32[]{:S(2)}) async-start(bf16[32,160,256]{2,1,0:T(8,128)(2,1)} %sort_by_owner.1), calls=%async_computation | async-start | bytes 5242880 | tf_op jit(solution)/shard_map/all_to_all | solution.py:372
  19.1 65.7 %collective-permute-start.1 = (f32[256,128]{1,0:T(8,128)S(1)}, f32[256,128]{1,0:T(8,128)S(1)}, u32[]{:S(2)}, u32[]{:S(2)}) collective-permute-start(f32[256,128]{1,0:T(8,128)S(1)} %add.33), channel_id=1, source_target_pairs={{0,16},{1,17},{2,18},{3,19},{4,20},{5,21},{6,22},{7,23},{8,24},{9,... | collective-permute-start | bytes 393224 | tf_op jit(solution)/shard_map/ppermute | solution.py:341
  84.8 1.3 %collective-permute-start.2 = (f32[128,128]{1,0:T(8,128)S(1)}, f32[128,128]{1,0:T(8,128)S(1)}, u32[]{:S(2)}, u32[]{:S(2)}) collective-permute-start(f32[128,128]{1,0:T(8,128)S(1)} %constant_dynamic-slice_fusion.2), channel_id=1, source_target_pairs={{0,1},{1,0},{2,3},{3,2},{4,5},{5,4},{6,7},{7,6},{8,9},{9,8},{10,11... | collective-permute-start | bytes 196616 | tf_op jit(solution)/shard_map/ppermute | solution.py:341
  86.2 4.0 %collective-permute-start.3 = (f32[64,128]{1,0:T(8,128)S(1)}, f32[64,128]{1,0:T(8,128)S(1)}, u32[]{:S(2)}, u32[]{:S(2)}) collective-permute-start(f32[64,128]{1,0:T(8,128)S(1)} %constant_dynamic-slice_fusion.1), channel_id=1, source_target_pairs={{0,2},{1,3},{2,0},{3,1},{4,6},{5,7},{6,4},{7,5},{8,10},{9,11},{10,... | collective-permute-start | bytes 98312 | tf_op jit(solution)/shard_map/ppermute | solution.py:341
  90.2 3.8 %collective-permute-start.4 = (f32[32,128]{1,0:T(8,128)S(1)}, f32[32,128]{1,0:T(8,128)S(1)}, u32[]{:S(2)}, u32[]{:S(2)}) collective-permute-start(f32[32,128]{1,0:T(8,128)S(1)} %constant_dynamic-slice_fusion), channel_id=1, source_target_pairs={{0,4},{1,5},{2,6},{3,7},{4,0},{5,1},{6,2},{7,3},{8,12},{9,13},{10,... | collective-permute-start | bytes 49160 | tf_op jit(solution)/shard_map/ppermute | solution.py:341
  94.0 3.7 %collective-permute-start.5 = (f32[32,128]{1,0:T(8,128)S(1)}, f32[32,128]{1,0:T(8,128)S(1)}, u32[]{:S(2)}, u32[]{:S(2)}) collective-permute-start(f32[32,128]{1,0:T(8,128)S(1)} %dynamic-slice_add_fusion.2), channel_id=1, source_target_pairs={{0,4},{1,5},{2,6},{3,7},{4,0},{5,1},{6,2},{7,3},{8,12},{9,13},{10,... | collective-permute-start | bytes 49160 | tf_op jit(solution)/shard_map/ppermute | solution.py:341
  97.7 3.9 %collective-permute-start.6 = (f32[64,128]{1,0:T(8,128)S(1)}, f32[64,128]{1,0:T(8,128)S(1)}, u32[]{:S(2)}, u32[]{:S(2)}) collective-permute-start(f32[64,128]{1,0:T(8,128)S(1)} %maximum_select_fusion.2), channel_id=1, source_target_pairs={{0,2},{1,3},{2,0},{3,1},{4,6},{5,7},{6,4},{7,5},{8,10},{9,11},{10,... | collective-permute-start | bytes 98312 | tf_op jit(solution)/shard_map/ppermute | solution.py:341
  101.7 1.3 %collective-permute-start.7 = (f32[128,128]{1,0:T(8,128)S(1)}, f32[128,128]{1,0:T(8,128)S(1)}, u32[]{:S(2)}, u32[]{:S(2)}) collective-permute-start(f32[128,128]{1,0:T(8,128)S(1)} %maximum_select_fusion.1), channel_id=1, source_target_pairs={{0,1},{1,0},{2,3},{3,2},{4,5},{5,4},{6,7},{7,6},{8,9},{9,8},{10,11... | collective-permute-start | bytes 196616 | tf_op jit(solution)/shard_map/ppermute | solution.py:341
where the time goes:
time: 125 us; the launch traced here: 124 us
  waiting for transfers between devices  75.1 us (60%)
  Pallas kernels  30.6 us (24%)
  starting transfers between devices  16.6 us (13%)
  local copies, waits for them, and re-layouts  1.28 us (1%)
    ppermute x8, waiting for transfers between devices, swap(): return lax.ppermute(x, 'rows', [(i, i ^ reach) for i in range(n)])  75.1 us
    pallas_call x1, Pallas kernels, small_algebra(): pl.pallas_call(functools.partial(small_kernel, rank, count), in_specs=[vm...  12.2 us
    ppermute x8, starting transfers between devices, swap(): return lax.ppermute(x, 'rows', [(i, i ^ reach) for i in range(n)])  11.7 us
    pallas_call x1, Pallas kernels, right_products(): pl.pallas_call(right_kernel, grid=(local // wide,), in_specs=[spec(rank),...  5.46 us
    pallas_call x1, Pallas kernels, sort_by_owner(): pl.pallas_call(functools.partial(sort_kernel, n), grid=(chunks,), in_spec...  5.32 us
    all_to_all x1, starting transfers between devices, shards(): lax.all_to_all(mine, 'rows', split_axis=0, concat_axis=0, tiled=True)  4.85 us
    pallas_call x1, Pallas kernels, packed_grams(): pl.pallas_call(gram_kernel, grid=(local // wide,), in_specs=[spec(rank),...  4.42 us
    pallas_call x1, Pallas kernels, left_products(): pl.pallas_call(left_kernel, grid=(n // group,), in_specs=[pl.BlockSpec((g...  3.17 us
  transfers between devices with their start and end apart: 9, of which 7 were waited for; matrix products, arithmetic and copies ran while one was open for 0% of the time, Pallas kernels for 18%

commit v1 on v0

--- a/solution.py
+++ b/solution.py
@@ -39,9 +39,8 @@
     return x.astype(HALF).astype(SINGLE)
 
 
-def sort_kernel(n, p_ref, w_ref, out_ref, turned):
-    cross = out_ref.shape[1]
-    wide = p_ref.shape[1]
+def sort_kernel(n, x_ref, out_ref, turned, ready, sem):
+    cross, local = x_ref.shape
     tile = SORT_TILE
     runs = tile // n
     row, column = iota((tile, tile), 0), iota((tile, tile), 1)
@@ -49,74 +48,94 @@
     permutation = jnp.where(column == wanted, 1.0, 0.0).astype(HALF)
     eye = jnp.where(iota((cross, cross), 0) == iota((cross, cross), 1), 1.0, 0.0).astype(HALF)
     pair = 16 // runs if runs < 16 else 1
-    for at in range(0, wide, tile * pair):
+    for at in range(0, local, tile * pair):
         parts = []
         for i in range(pair):
-            cut = slice(at + i * tile, at + (i + 1) * tile)
-            both = jnp.concatenate([p_ref[:, cut].astype(SINGLE), w_ref[:, cut].astype(SINGLE)], 0)
-            part = lax.dot_general(permutation, both.astype(HALF), NT, preferred_element_type=SINGLE)
+            x = x_ref[:, at + i * tile : at + (i + 1) * tile]
+            part = lax.dot_general(permutation, x, NT, preferred_element_type=SINGLE)
             parts.append(part.reshape(n, runs, cross))
         rows = slice(at // n, at // n + runs * pair)
         turned[:, rows, :] = jnp.concatenate(parts, 1).astype(HALF)
+    copies = []
     for owner in range(n):
         mine = lax.dot_general(eye, turned[owner], NT, preferred_element_type=SINGLE)
-        out_ref[owner] = mine.astype(HALF)
-
-
-def sort_by_owner(p_left, w_cols, n):
-    rank, local = p_left.shape
-    cols = w_cols.shape[0]
+        ready[owner] = mine.astype(HALF)
+        copies.append(pltpu.make_async_copy(ready.at[owner], out_ref.at[owner], sem.at[owner]))
+        copies[-1].start()
+    for copy in copies:
+        copy.wait()
+
+
+def sort_by_owner(x, n):
+    cross, local = x.shape
     share = local // n
-    chunks = share // LANES if share % LANES == 0 else 1
-    wide = local // chunks
     return pl.pallas_call(
         functools.partial(sort_kernel, n),
-        grid=(chunks,),
-        in_specs=[
-            pl.BlockSpec((rank, wide), lambda i: (0, i)),
-            pl.BlockSpec((cols, wide), lambda i: (0, i)),
-        ],
-        out_specs=pl.BlockSpec((n, rank + cols, share // chunks), lambda i: (0, 0, i)),
-        out_shape=pltpu.HBM((n, rank + cols, share), HALF),
-        scratch_shapes=[pltpu.VMEM((n, share // chunks, rank + cols), HALF)],
+        in_specs=[pl.BlockSpec(memory_space=pltpu.VMEM)],
+        out_specs=pl.BlockSpec(memory_space=pltpu.HBM),
+        out_shape=pltpu.HBM((n, cross, share), HALF),
+        scratch_shapes=[
+            pltpu.VMEM((n, share, cross), HALF),
+            pltpu.VMEM((n, cross, share), HALF),
+            pltpu.SemaphoreType.DMA((n,)),
+        ],
         compiler_params=pltpu.CompilerParams(vmem_limit_bytes=VMEM_LIMIT),
         name="sort_by_owner",
-    )(*in_hbm(p_left, w_cols))
-
-
-def gram_kernel(p_ref, w_ref, phi_ref, v_ref, res_ref, out_ref, left, right):
-    at = pl.program_id(0)
-
-    @pl.when(at == 0)
-    def _():
-        left[...] = jnp.zeros_like(left)
-        right[...] = jnp.zeros_like(right)
-
-    x = jnp.concatenate([p_ref[...].astype(SINGLE), w_ref[...].astype(SINGLE)], 0).astype(HALF)
-    left[...] += lax.dot_general(x, x, NT, preferred_element_type=SINGLE)
-    wide = res_ref.shape[1]
-    last = jnp.where(iota((8, wide), 0) == 0, res_ref[...].astype(SINGLE), 0.0)
-    y = jnp.concatenate([phi_ref[...].astype(SINGLE), v_ref[...].astype(SINGLE), last], 0).astype(HALF)
-    right[...] += lax.dot_general(y, y, NT, preferred_element_type=SINGLE)
-
-    @pl.when(at == pl.num_programs(0) - 1)
-    def _():
-        cross = left.shape[0]
-        m = LANES
-        e = cross - m
-        rows, lanes = iota((m, m), 0), iota((m, m), 1)
-        top_right = right[0:m, 0:m]
-        out_ref[0:m, :] = jnp.where(lanes <= rows, left[0:m, 0:m], top_right)
-        out_ref[m : m + e, :] = left[m:cross, 0:m]
-        out_ref[m + e : m + 2 * e, :] = right[m:cross, 0:m]
-        out_ref[m + 2 * e : m + 3 * e, :] = jnp.zeros((e, m), SINGLE)
-        out_ref[m + 2 * e : m + 3 * e, 0:e] = left[m:cross, m:cross]
-        out_ref[m + 2 * e : m + 3 * e, e : 2 * e] = right[m:cross, m:cross]
-        base = m + 3 * e
-        out_ref[base:, :] = jnp.zeros((out_ref.shape[0] - base, m), SINGLE)
-        out_ref[base : base + 1, :] = jnp.sum(jnp.where(rows == lanes, top_right, 0.0), 0, keepdims=True)
-        out_ref[base + 1 : base + 2, :] = right[cross : cross + 1, 0:m]
-        out_ref[base + 2 : base + 3, 0 : e + 1] = right[cross : cross + 1, m : cross + 1]
+    )(in_vmem(x))
+
+
+def gram_kernel(chunks, p_hbm, w_hbm, phi_hbm, v_hbm, res_hbm, out_ref, x_ref, *scratch):
+    *buffers, left, right, sem = scratch
+    sources = (p_hbm, w_hbm, phi_hbm, v_hbm)
+    wide = x_ref.shape[1] // chunks
+    res_buffer = buffers[-1]
+    res_copy = pltpu.make_async_copy(res_hbm, res_buffer, sem.at[len(sources), 0])
+    copies = []
+    for at in range(chunks):
+        cut = pl.ds(at * wide, wide)
+        copies.append(
+            [
+                pltpu.make_async_copy(source.at[:, cut], buffer.at[:, cut], sem.at[i, at])
+                for i, (source, buffer) in enumerate(zip(sources, buffers))
+            ]
+        )
+        for copy in copies[-1]:
+            copy.start()
+        if at == 0:
+            res_copy.start()
+    for at in range(chunks):
+        cut = slice(at * wide, (at + 1) * wide)
+        for copy in copies[at]:
+            copy.wait()
+        if at == 0:
+            res_copy.wait()
+        p, w, phi, v = [buffer[:, cut].astype(SINGLE) for buffer in buffers[:4]]
+        x = jnp.concatenate([p, w], 0).astype(HALF)
+        x_ref[:, cut] = x
+        more = lax.dot_general(x, x, NT, preferred_element_type=SINGLE)
+        left[...] = more if at == 0 else left[...] + more
+        y = jnp.concatenate([phi, v], 0).astype(HALF)
+        res = res_buffer[cut].astype(SINGLE).reshape(1, wide)
+        last = jnp.where(iota((16, wide), 0) == 0, res, 0.0).astype(HALF)
+        z = jnp.concatenate([y, last], 0)
+        more = lax.dot_general(z, z, NT, preferred_element_type=SINGLE)
+        right[...] = more if at == 0 else right[...] + more
+    cross = left.shape[0]
+    m = LANES
+    e = cross - m
+    rows, lanes = iota((m, m), 0), iota((m, m), 1)
+    top_right = right[0:m, 0:m]
+    out_ref[0:m, :] = jnp.where(lanes <= rows, left[0:m, 0:m], top_right)
+    out_ref[m : m + e, :] = left[m:cross, 0:m]
+    out_ref[m + e : m + 2 * e, :] = right[m:cross, 0:m]
+    out_ref[m + 2 * e : m + 3 * e, :] = jnp.zeros((e, m), SINGLE)
+    out_ref[m + 2 * e : m + 3 * e, 0:e] = left[m:cross, m:cross]
+    out_ref[m + 2 * e : m + 3 * e, e : 2 * e] = right[m:cross, m:cross]
+    base = m + 3 * e
+    out_ref[base:, :] = jnp.zeros((out_ref.shape[0] - base, m), SINGLE)
+    out_ref[base : base + 1, :] = jnp.sum(jnp.where(rows == lanes, top_right, 0.0), 0, keepdims=True)
+    out_ref[base + 1 : base + 2, :] = right[cross : cross + 1, 0:m]
+    out_ref[base + 2 : base + 3, 0 : e + 1] = right[cross : cross + 1, m : cross + 1]
 
 
 def packed_rows(cross):
@@ -128,18 +147,30 @@
     rank, local = p_left.shape
     cols = w_cols.shape[0]
     cross = rank + cols
-    wide = min(local, 2048)
-    spec = lambda rows: pl.BlockSpec((rows, wide), lambda i: (0, i))
+    chunks = 4
+    hbm = pl.BlockSpec(memory_space=pltpu.HBM)
+    vmem = pl.BlockSpec(memory_space=pltpu.VMEM)
     return pl.pallas_call(
-        gram_kernel,
-        grid=(local // wide,),
-        in_specs=[spec(rank), spec(cols), spec(rank), spec(cols), spec(1)],
-        out_specs=pl.BlockSpec((packed_rows(cross), LANES), lambda i: (0, 0)),
-        out_shape=pltpu.VMEM((packed_rows(cross), LANES), SINGLE),
-        scratch_shapes=[pltpu.VMEM((cross, cross), SINGLE), pltpu.VMEM((cross + 8, cross + 8), SINGLE)],
+        functools.partial(gram_kernel, chunks),
+        in_specs=[hbm] * 5,
+        out_specs=[vmem] * 2,
+        out_shape=[
+            pltpu.VMEM((packed_rows(cross), LANES), SINGLE),
+            pltpu.VMEM((cross, local), HALF),
+        ],
+        scratch_shapes=[
+            pltpu.VMEM((rank, local), HALF),
+            pltpu.VMEM((cols, local), HALF),
+            pltpu.VMEM((rank, local), HALF),
+            pltpu.VMEM((cols, local), HALF),
+            pltpu.VMEM((local,), HALF),
+            pltpu.VMEM((cross, cross), SINGLE),
+            pltpu.VMEM((cross + 16, cross + 16), SINGLE),
+            pltpu.SemaphoreType.DMA((5, chunks)),
+        ],
         compiler_params=pltpu.CompilerParams(vmem_limit_bytes=VMEM_LIMIT),
         name="packed_grams",
-    )(*in_hbm(p_left, w_cols, phi_right, v_cols), residual.reshape(1, local))
+    )(*in_hbm(p_left, w_cols, phi_right, v_cols, residual))
 
 
 def eliminate(refs, tops, k):
@@ -305,7 +336,7 @@
         out_specs=[spec(1), spec(cross)],
         out_shape=[
             jax.ShapeDtypeStruct((1, local), SINGLE),
-            jax.ShapeDtypeStruct((cross, local), HALF),
+            pltpu.HBM((cross, local), HALF),
         ],
         compiler_params=pltpu.CompilerParams(vmem_limit_bytes=VMEM_LIMIT),
         name="right_products",
@@ -341,20 +372,18 @@
     return lax.ppermute(x, "rows", [(i, i ^ reach) for i in range(n)])
 
 
-def sum_over_rest(x, reaches):
-    me = lax.axis_index("rows")
-    splits = []
-    for reach in reaches:
-        half = x.shape[0] // 2
-        bit = lax.rem(lax.div(me, reach), 2)
-        kept = lax.dynamic_slice_in_dim(x, bit * half, half)
-        given = lax.dynamic_slice_in_dim(x, (1 - bit) * half, half)
-        x = kept + swap(given, reach)
-        splits.append((reach, bit))
-    for reach, bit in reversed(splits):
-        other = swap(x, reach)
-        x = jnp.where(bit == 0, jnp.concatenate([x, other], 0), jnp.concatenate([other, x], 0))
-    return x
+def split(x, reach):
+    half = x.shape[0] // 2
+    bit = lax.rem(lax.div(lax.axis_index("rows"), reach), 2)
+    kept = lax.dynamic_slice_in_dim(x, bit * half, half)
+    given = lax.dynamic_slice_in_dim(x, (1 - bit) * half, half)
+    return kept + swap(given, reach)
+
+
+def join(x, reach):
+    bit = lax.rem(lax.div(lax.axis_index("rows"), reach), 2)
+    other = swap(x, reach)
+    return jnp.where(bit == 0, jnp.concatenate([x, other], 0), jnp.concatenate([other, x], 0))
 
 
 def shards(p_left, phi_right, v_cols, w_cols, residual):
@@ -363,15 +392,19 @@
     n = lax.axis_size("rows")
     near = [1 << i for i in range(3)]
     far = [1 << i for i in range(3, n.bit_length() - 1)]
-    packed = packed_grams(p_left, w_cols, phi_right, v_cols, residual)
-    mine = sort_by_owner(p_left, w_cols, n)
+    packed, x = packed_grams(p_left, w_cols, phi_right, v_cols, residual)
+    packed = split(packed, near[0])
+    mine = sort_by_owner(x, n)
     for reach in far[:-1]:
         packed = packed + swap(packed, reach)
     mine, packed = lax.optimization_barrier((mine, packed))
     other = swap(packed, far[-1])
     owned = lax.all_to_all(mine, "rows", split_axis=0, concat_axis=0, tiled=True)
     packed = packed + other
-    packed = sum_over_rest(packed, near)
+    for reach in near[1:]:
+        packed = split(packed, reach)
+    for reach in reversed(near):
+        packed = join(packed, reach)
     k_left, k_right, u, rms = small_algebra(packed, rank, cols, float(local * n))
     update, q_right = right_products(p_left, w_cols, phi_right, v_cols, k_right, u)
     q_left = left_products(owned, k_left)

time: 125 us -> 119 us (0.952)
  waiting for transfers between devices: 75.1 us -> 72.2 us
  Pallas kernels: 30.6 us -> 28.3 us
    ppermute x8, waiting for transfers between devices: 75.1 us -> 72.2 us  [swap(): return lax.ppermute(x, 'rows', [(i, i ^ reach) for i in range(n)])]
    pallas_call x2, Pallas kernels: 9.74 us -> 7.47 us  [the longest x1 3.82 us: packed_grams(): pl.pallas_call(functools.partial(gram_kernel, chunks), in_specs=[hbm] * 5...]
where the time goes in v1:
time: 119 us
  waiting for transfers between devices  72.2 us (61%)
  Pallas kernels  28.3 us (24%)
  starting transfers between devices  16.9 us (14%)
    ppermute x8, waiting for transfers between devices, swap(): return lax.ppermute(x, 'rows', [(i, i ^ reach) for i in range(n)])  72.2 us
    pallas_call x1, Pallas kernels, small_algebra(): pl.pallas_call(functools.partial(small_kernel, rank, count), in_specs=[vm...  12.2 us
    ppermute x8, starting transfers between devices, swap(): return lax.ppermute(x, 'rows', [(i, i ^ reach) for i in range(n)])  12 us
    pallas_call x1, Pallas kernels, right_products(): pl.pallas_call(right_kernel, grid=(local // wide,), in_specs=[spec(rank),...  5.46 us
    all_to_all x1, starting transfers between devices, shards(): lax.all_to_all(mine, 'rows', split_axis=0, concat_axis=0, tiled=True)  4.87 us
    pallas_call x1, Pallas kernels, packed_grams(): pl.pallas_call(functools.partial(gram_kernel, chunks), in_specs=[hbm] * 5...  3.82 us
    pallas_call x1, Pallas kernels, sort_by_owner(): pl.pallas_call(functools.partial(sort_kernel, n), in_specs=[pl.BlockSpec(...  3.65 us
    pallas_call x1, Pallas kernels, left_products(): pl.pallas_call(left_kernel, grid=(n // group,), in_specs=[pl.BlockSpec((g...  3.17 us
  transfers between devices with their start and end apart: 9, of which 7 were waited for; matrix products, arithmetic and copies ran while one was open for 0% of the time, Pallas kernels for 18%

profile of v1, /device:TPU:0, one launch (start us, length us, event | category | flops | bytes accessed | tf_op | source)
XLA Modules:
  0.0 118.7 jit_solution(3044060318219035673)
XLA Ops:
  0.6 3.8 %packed_grams.1 = (f32[256,128]{1,0:T(8,128)S(1)}, bf16[160,8192]{1,0:T(8,128)(2,1)S(1)}) custom-call(bf16[120,8192]{1,0:T(8,128)(2,1)} %p_ref.1, bf16[40,8192]{1,0:T(8,128)(2,1)} %w_ref.1, bf16[120,8192]{1,0:T(8,128)(2,1)} %phi_ref.1, bf16[40,8192]{1,0:T(8,128)(2,1)} %v_ref.1, bf16[8192]{0:T(1024)(128)(2,1)} %res_hbm.1), custom_call_target="tpu_custom_call" | custom-call | tf_op jit(solution)/shard_map/packed_grams/pallas_call | solution.py:153
  4.5 0.6 collective-permute-start
  5.0 0.9 collective-permute-done
  6.0 3.0 %collective-permute-start.1 = (f32[128,128]{1,0:T(8,128)S(1)}, f32[128,128]{1,0:T(8,128)S(1)}, u32[]{:S(2)}, u32[]{:S(2)}) collective-permute-start(f32[128,128]{1,0:T(8,128)S(1)} %dynamic-slice_add_fusion), channel_id=1, source_target_pairs={{0,8},{1,9},{2,10},{3,11},{4,12},{5,13},{6,14},{7,15},{8,0},{9,1},... | collective-permute-start | bytes 196616 | tf_op jit(solution)/shard_map/ppermute | solution.py:372
  8.9 3.6 %sort_by_owner.1 = bf16[32,160,256]{2,1,0:T(8,128)(2,1)} custom-call(bf16[160,8192]{1,0:T(8,128)(2,1)S(1)} %get-tuple-element.14.x_ref), custom_call_target="tpu_custom_call" | custom-call | tf_op jit(solution)/shard_map/sort_by_owner/pallas_call | solution.py:72
  12.6 0.0 collective-permute-done.1
  12.6 4.9 %all-to-all-start = ((bf16[32,160,256]{2,1,0:T(8,128)(2,1)}), bf16[32,160,256]{2,1,0:T(8,128)(2,1)S(1)}, u32[]{:S(2)}, u32[]{:S(2)}) async-start(bf16[32,160,256]{2,1,0:T(8,128)(2,1)} %sort_by_owner.1), calls=%async_computation | async-start | bytes 5242880 | tf_op jit(solution)/shard_map/all_to_all | solution.py:402
  17.5 2.7 %collective-permute-start.2 = (f32[128,128]{1,0:T(8,128)S(1)}, f32[128,128]{1,0:T(8,128)S(1)}, u32[]{:S(2)}, u32[]{:S(2)}) collective-permute-start(f32[128,128]{1,0:T(8,128)S(1)} %add.36), channel_id=1, source_target_pairs={{0,16},{1,17},{2,18},{3,19},{4,20},{5,21},{6,22},{7,23},{8,24},{9,... | collective-permute-start | bytes 196616 | tf_op jit(solution)/shard_map/ppermute | solution.py:372
  20.2 60.1 %collective-permute-done.2 = f32[128,128]{1,0:T(8,128)S(1)} collective-permute-done((f32[128,128]{1,0:T(8,128)S(1)}, f32[128,128]{1,0:T(8,128)S(1)}, u32[]{:S(2)}, u32[]{:S(2)}) %collective-permute-start.2) | collective-permute-done | bytes 65568 | tf_op jit(solution)/shard_map/ppermute | solution.py:372
  80.4 1.5 %collective-permute-start.3 = (f32[64,128]{1,0:T(8,128)S(1)}, f32[64,128]{1,0:T(8,128)S(1)}, u32[]{:S(2)}, u32[]{:S(2)}) collective-permute-start(f32[64,128]{1,0:T(8,128)S(1)} %constant_dynamic-slice_fusion.1), channel_id=1, source_target_pairs={{0,2},{1,3},{2,0},{3,1},{4,6},{5,7},{6,4},{7,5},{8,10},{9,11},{10,... | collective-permute-start | bytes 98312 | tf_op jit(solution)/shard_map/ppermute | solution.py:372
  81.9 2.5 %collective-permute-done.3 = f32[64,128]{1,0:T(8,128)S(1)} collective-permute-done((f32[64,128]{1,0:T(8,128)S(1)}, f32[64,128]{1,0:T(8,128)S(1)}, u32[]{:S(2)}, u32[]{:S(2)}) %collective-permute-start.3) | collective-permute-done | bytes 32800 | tf_op jit(solution)/shard_map/ppermute | solution.py:372
  84.4 1.4 %collective-permute-start.4 = (f32[32,128]{1,0:T(8,128)S(1)}, f32[32,128]{1,0:T(8,128)S(1)}, u32[]{:S(2)}, u32[]{:S(2)}) collective-permute-start(f32[32,128]{1,0:T(8,128)S(1)} %constant_dynamic-slice_fusion), channel_id=1, source_target_pairs={{0,4},{1,5},{2,6},{3,7},{4,0},{5,1},{6,2},{7,3},{8,12},{9,13},{10,... | collective-permute-start | bytes 49160 | tf_op jit(solution)/shard_map/ppermute | solution.py:372
  85.8 2.6 %collective-permute-done.4 = f32[32,128]{1,0:T(8,128)S(1)} collective-permute-done((f32[32,128]{1,0:T(8,128)S(1)}, f32[32,128]{1,0:T(8,128)S(1)}, u32[]{:S(2)}, u32[]{:S(2)}) %collective-permute-start.4) | collective-permute-done | bytes 16416 | tf_op jit(solution)/shard_map/ppermute | solution.py:372
  88.4 1.3 %collective-permute-start.5 = (f32[32,128]{1,0:T(8,128)S(1)}, f32[32,128]{1,0:T(8,128)S(1)}, u32[]{:S(2)}, u32[]{:S(2)}) collective-permute-start(f32[32,128]{1,0:T(8,128)S(1)} %dynamic-slice_add_fusion.2), channel_id=1, source_target_pairs={{0,4},{1,5},{2,6},{3,7},{4,0},{5,1},{6,2},{7,3},{8,12},{9,13},{10,... | collective-permute-start | bytes 49160 | tf_op jit(solution)/shard_map/ppermute | solution.py:372
  89.7 2.4 %collective-permute-done.5 = f32[32,128]{1,0:T(8,128)S(1)} collective-permute-done((f32[32,128]{1,0:T(8,128)S(1)}, f32[32,128]{1,0:T(8,128)S(1)}, u32[]{:S(2)}, u32[]{:S(2)}) %collective-permute-start.5) | collective-permute-done | bytes 16416 | tf_op jit(solution)/shard_map/ppermute | solution.py:372
  92.1 1.5 %collective-permute-start.6 = (f32[64,128]{1,0:T(8,128)S(1)}, f32[64,128]{1,0:T(8,128)S(1)}, u32[]{:S(2)}, u32[]{:S(2)}) collective-permute-start(f32[64,128]{1,0:T(8,128)S(1)} %maximum_select_fusion.2), channel_id=1, source_target_pairs={{0,2},{1,3},{2,0},{3,1},{4,6},{5,7},{6,4},{7,5},{8,10},{9,11},{10,... | collective-permute-start | bytes 98312 | tf_op jit(solution)/shard_map/ppermute | solution.py:372
  93.6 2.5 %collective-permute-done.6 = f32[64,128]{1,0:T(8,128)S(1)} collective-permute-done((f32[64,128]{1,0:T(8,128)S(1)}, f32[64,128]{1,0:T(8,128)S(1)}, u32[]{:S(2)}, u32[]{:S(2)}) %collective-permute-start.6) | collective-permute-done | bytes 32800 | tf_op jit(solution)/shard_map/ppermute | solution.py:372
  96.0 0.1 collective-permute-start.7
  96.1 1.2 %collective-permute-done.7 = f32[128,128]{1,0:T(8,128)S(1)} collective-permute-done((f32[128,128]{1,0:T(8,128)S(1)}, f32[128,128]{1,0:T(8,128)S(1)}, u32[]{:S(2)}, u32[]{:S(2)}) %collective-permute-start.7) | collective-permute-done | bytes 65568 | tf_op jit(solution)/shard_map/ppermute | solution.py:372
  97.4 12.2 %small_algebra.1 = (bf16[320,160]{1,0:T(8,128)(2,1)S(1)}, bf16[320,160]{1,0:T(8,128)(2,1)S(1)}, f32[8,160]{1,0:T(8,128)S(1)}, f32[1,128]{1,0:T(1,128)S(1)}) custom-call(f32[256,128]{1,0:T(8,128)S(1)} %maximum_select_fusion.g_ref), custom_call_target="tpu_custom_call" | custom-call | tf_op jit(solution)/shard_map/small_algebra/pallas_call | solution.py:291
  109.6 5.5 %right_products.1 = (f32[1,8192]{1,0:T(1,128)}, bf16[160,8192]{1,0:T(8,128)(2,1)}) custom-call(bf16[120,8192]{1,0:T(8,128)(2,1)} %p_ref.1, bf16[40,8192]{1,0:T(8,128)(2,1)} %w_ref.1, bf16[120,8192]{1,0:T(8,128)(2,1)} %phi_ref.1, bf16[40,8192]{1,0:T(8,128)(2,1)} %v_ref.1, bf16[320,160]{1,0:T(8,128)(2,1)S(1)} %get-tuple-element.17.k_ref, ...), custom_call_target="tpu_custom_call" | custom-call | tf_op jit(solution)/shard_map/right_products/pallas_call | solution.py:328
  115.0 0.5 slice_bitcast_fusion
  115.5 0.0 all-to-all-done.x_ref
  115.6 3.2 %left_products.1 = bf16[160,8192]{1,0:T(8,128)(2,1)} custom-call(bf16[32,160,256]{2,1,0:T(8,128)(2,1)S(1)} %all-to-all-done.x_ref, bf16[320,160]{1,0:T(8,128)(2,1)S(1)} %get-tuple-element.21.k_ref), custom_call_target="tpu_custom_call" | custom-call | tf_op jit(solution)/shard_map/left_products/pallas_call | solution.py:356
  (11 shorter events, 0.1 us)
Async XLA Ops:
  4.5 1.5 %collective-permute-start = (f32[128,128]{1,0:T(8,128)S(1)}, f32[128,128]{1,0:T(8,128)S(1)}, u32[]{:S(2)}, u32[]{:S(2)}) collective-permute-start(f32[128,128]{1,0:T(8,128)S(1)} %constant_dynamic-slice_fusion.2), channel_id=1, source_target_pairs={{0,1},{1,0},{2,3},{3,2},{4,5},{5,4},{6,7},{7,6},{8,9},{9,8},{10,11... | collective-permute-start | bytes 196616 | tf_op jit(solution)/shard_map/ppermute | solution.py:372
  6.0 6.6 %collective-permute-start.1 = (f32[128,128]{1,0:T(8,128)S(1)}, f32[128,128]{1,0:T(8,128)S(1)}, u32[]{:S(2)}, u32[]{:S(2)}) collective-permute-start(f32[128,128]{1,0:T(8,128)S(1)} %dynamic-slice_add_fusion), channel_id=1, source_target_pairs={{0,8},{1,9},{2,10},{3,11},{4,12},{5,13},{6,14},{7,15},{8,0},{9,1},... | collective-permute-start | bytes 196616 | tf_op jit(solution)/shard_map/ppermute | solution.py:372
  12.6 102.9 %all-to-all-start = ((bf16[32,160,256]{2,1,0:T(8,128)(2,1)}), bf16[32,160,256]{2,1,0:T(8,128)(2,1)S(1)}, u32[]{:S(2)}, u32[]{:S(2)}) async-start(bf16[32,160,256]{2,1,0:T(8,128)(2,1)} %sort_by_owner.1), calls=%async_computation | async-start | bytes 5242880 | tf_op jit(solution)/shard_map/all_to_all | solution.py:402
  17.5 62.9 %collective-permute-start.2 = (f32[128,128]{1,0:T(8,128)S(1)}, f32[128,128]{1,0:T(8,128)S(1)}, u32[]{:S(2)}, u32[]{:S(2)}) collective-permute-start(f32[128,128]{1,0:T(8,128)S(1)} %add.36), channel_id=1, source_target_pairs={{0,16},{1,17},{2,18},{3,19},{4,20},{5,21},{6,22},{7,23},{8,24},{9,... | collective-permute-start | bytes 196616 | tf_op jit(solution)/shard_map/ppermute | solution.py:372
  80.4 4.0 %collective-permute-start.3 = (f32[64,128]{1,0:T(8,128)S(1)}, f32[64,128]{1,0:T(8,128)S(1)}, u32[]{:S(2)}, u32[]{:S(2)}) collective-permute-start(f32[64,128]{1,0:T(8,128)S(1)} %constant_dynamic-slice_fusion.1), channel_id=1, source_target_pairs={{0,2},{1,3},{2,0},{3,1},{4,6},{5,7},{6,4},{7,5},{8,10},{9,11},{10,... | collective-permute-start | bytes 98312 | tf_op jit(solution)/shard_map/ppermute | solution.py:372
  84.4 4.0 %collective-permute-start.4 = (f32[32,128]{1,0:T(8,128)S(1)}, f32[32,128]{1,0:T(8,128)S(1)}, u32[]{:S(2)}, u32[]{:S(2)}) collective-permute-start(f32[32,128]{1,0:T(8,128)S(1)} %constant_dynamic-slice_fusion), channel_id=1, source_target_pairs={{0,4},{1,5},{2,6},{3,7},{4,0},{5,1},{6,2},{7,3},{8,12},{9,13},{10,... | collective-permute-start | bytes 49160 | tf_op jit(solution)/shard_map/ppermute | solution.py:372
  88.4 3.7 %collective-permute-start.5 = (f32[32,128]{1,0:T(8,128)S(1)}, f32[32,128]{1,0:T(8,128)S(1)}, u32[]{:S(2)}, u32[]{:S(2)}) collective-permute-start(f32[32,128]{1,0:T(8,128)S(1)} %dynamic-slice_add_fusion.2), channel_id=1, source_target_pairs={{0,4},{1,5},{2,6},{3,7},{4,0},{5,1},{6,2},{7,3},{8,12},{9,13},{10,... | collective-permute-start | bytes 49160 | tf_op jit(solution)/shard_map/ppermute | solution.py:372
  92.1 3.9 %collective-permute-start.6 = (f32[64,128]{1,0:T(8,128)S(1)}, f32[64,128]{1,0:T(8,128)S(1)}, u32[]{:S(2)}, u32[]{:S(2)}) collective-permute-start(f32[64,128]{1,0:T(8,128)S(1)} %maximum_select_fusion.2), channel_id=1, source_target_pairs={{0,2},{1,3},{2,0},{3,1},{4,6},{5,7},{6,4},{7,5},{8,10},{9,11},{10,... | collective-permute-start | bytes 98312 | tf_op jit(solution)/shard_map/ppermute | solution.py:372
  96.0 1.3 %collective-permute-start.7 = (f32[128,128]{1,0:T(8,128)S(1)}, f32[128,128]{1,0:T(8,128)S(1)}, u32[]{:S(2)}, u32[]{:S(2)}) collective-permute-start(f32[128,128]{1,0:T(8,128)S(1)} %maximum_select_fusion.1), channel_id=1, source_target_pairs={{0,1},{1,0},{2,3},{3,2},{4,5},{5,4},{6,7},{7,6},{8,9},{9,8},{10,11... | collective-permute-start | bytes 196616 | tf_op jit(solution)/shard_map/ppermute | solution.py:372

commit v2 on v1

--- a/solution.py
+++ b/solution.py
@@ -123,31 +123,36 @@
     cross = left.shape[0]
     m = LANES
     e = cross - m
-    rows, lanes = iota((m, m), 0), iota((m, m), 1)
     top_right = right[0:m, 0:m]
-    out_ref[0:m, :] = jnp.where(lanes <= rows, left[0:m, 0:m], top_right)
+    same = iota((m, m), 0) == iota((m, m), 1)
+    out_ref[0:m, :] = jnp.where(iota((m, m), 1) <= iota((m, m), 0), left[0:m, 0:m], top_right)
     out_ref[m : m + e, :] = left[m:cross, 0:m]
     out_ref[m + e : m + 2 * e, :] = right[m:cross, 0:m]
-    out_ref[m + 2 * e : m + 3 * e, :] = jnp.zeros((e, m), SINGLE)
-    out_ref[m + 2 * e : m + 3 * e, 0:e] = left[m:cross, m:cross]
-    out_ref[m + 2 * e : m + 3 * e, e : 2 * e] = right[m:cross, m:cross]
-    base = m + 3 * e
-    out_ref[base:, :] = jnp.zeros((out_ref.shape[0] - base, m), SINGLE)
-    out_ref[base : base + 1, :] = jnp.sum(jnp.where(rows == lanes, top_right, 0.0), 0, keepdims=True)
+    corner_right = right[m:cross, m:cross]
+    lower = iota((e, e), 1) <= iota((e, e), 0)
+    corner = jnp.where(lower, left[m:cross, m:cross], corner_right)
+    base = m + 2 * e
+    out_ref[base : base + 2 * BLOCK, :] = jnp.zeros((2 * BLOCK, m), SINGLE)
+    for i in range(e // BLOCK):
+        out_ref[base : base + BLOCK, i * e : (i + 1) * e] = corner[i * BLOCK : (i + 1) * BLOCK, :]
+    base += BLOCK
+    out_ref[base : base + 1, :] = jnp.sum(jnp.where(same, top_right, 0.0), 0, keepdims=True)
     out_ref[base + 1 : base + 2, :] = right[cross : cross + 1, 0:m]
     out_ref[base + 2 : base + 3, 0 : e + 1] = right[cross : cross + 1, m : cross + 1]
+    out_ref[base + 3 : base + 4, 0:e] = jnp.sum(
+        jnp.where(iota((e, e), 0) == iota((e, e), 1), corner_right, 0.0), 0, keepdims=True
+    )
 
 
 def packed_rows(cross):
-    used = LANES + 3 * (cross - LANES) + BLOCK
-    return -(-used // (8 * BLOCK)) * 8 * BLOCK
+    return LANES + 2 * (cross - LANES) + 2 * BLOCK
 
 
 def packed_grams(p_left, w_cols, phi_right, v_cols, residual):
     rank, local = p_left.shape
     cols = w_cols.shape[0]
     cross = rank + cols
-    chunks = 4
+    chunks = 2
     hbm = pl.BlockSpec(memory_space=pltpu.HBM)
     vmem = pl.BlockSpec(memory_space=pltpu.VMEM)
     return pl.pallas_call(
@@ -222,20 +227,27 @@
     cross = left.shape[0]
     m = LANES
     e = cross - m
-    base = m + 3 * e
-    rows, lanes = iota((m, m), 0), iota((m, m), 1)
-    top = g_ref[0:m, :]
-    lower = jnp.where(lanes < rows, top, 0.0)
-    upper = jnp.where(lanes > rows, top, 0.0)
-    same = rows == lanes
-    left[0:m, 0:m] = lower + lower.T + jnp.where(same, top, 0.0)
-    right[0:m, 0:m] = upper + upper.T + jnp.where(same, g_ref[base : base + 1, :], 0.0)
+    base = m + 2 * e + BLOCK
+
+    def unfold(packed, diagonal):
+        rows, lanes = iota(packed.shape, 0), iota(packed.shape, 1)
+        lower = jnp.where(lanes < rows, packed, 0.0)
+        upper = jnp.where(lanes > rows, packed, 0.0)
+        same = rows == lanes
+        return (
+            lower + lower.T + jnp.where(same, packed, 0.0),
+            upper + upper.T + jnp.where(same, diagonal, 0.0),
+        )
+
+    left[0:m, 0:m], right[0:m, 0:m] = unfold(g_ref[0:m, :], g_ref[base : base + 1, :])
     left[m:cross, 0:m] = g_ref[m : m + e, :]
     right[m:cross, 0:m] = g_ref[m + e : m + 2 * e, :]
     left[0:m, m:cross] = g_ref[m : m + e, :].T
     right[0:m, m:cross] = g_ref[m + e : m + 2 * e, :].T
-    left[m:cross, m:cross] = g_ref[m + 2 * e : m + 3 * e, 0:e]
-    right[m:cross, m:cross] = g_ref[m + 2 * e : m + 3 * e, e : 2 * e]
+    corner = jnp.concatenate(
+        [g_ref[base - BLOCK : base, i * e : (i + 1) * e] for i in range(e // BLOCK)], 0
+    )
+    left[m:cross, m:cross], right[m:cross, m:cross] = unfold(corner, g_ref[base + 3 : base + 4, 0:e])
     g_left = left[...]
     g_right = right[...]
     res_first = g_ref[base + 1 : base + 2, :]
@@ -343,25 +355,38 @@
     )(*in_hbm(p_left, w_cols, phi_right, v_cols), in_vmem(k_right), in_vmem(u))
 
 
-def left_kernel(x_ref, k_ref, q_ref):
-    group, cross, share = x_ref.shape
-    for i in range(group):
-        both = jnp.dot(k_ref[...], x_ref[i], preferred_element_type=SINGLE)
-        q_ref[:, i * share : (i + 1) * share] = (both[0:cross] + both[cross : 2 * cross]).astype(HALF)
+def left_kernel(x_ref, k_ref, q_ref, ready, sem):
+    n, cross, share = x_ref.shape
+    group = n // sem.shape[0]
+    wide = group * share
+    k = k_ref[...]
+    copies = []
+    for at in range(sem.shape[0]):
+        for i in range(group):
+            both = jnp.dot(k, x_ref[at * group + i], preferred_element_type=SINGLE)
+            ready[:, at * wide + i * share : at * wide + (i + 1) * share] = (
+                both[0:cross] + both[cross : 2 * cross]
+            ).astype(HALF)
+        cut = pl.ds(at * wide, wide)
+        copies.append(pltpu.make_async_copy(ready.at[:, cut], q_ref.at[:, cut], sem.at[at]))
+        copies[-1].start()
+    for copy in copies:
+        copy.wait()
 
 
 def left_products(sorted_x, k_left):
     n, cross, share = sorted_x.shape
-    group = max(1, 2048 // share)
+    group = max(1, 512 // share)
+    vmem = pl.BlockSpec(memory_space=pltpu.VMEM)
     return pl.pallas_call(
         left_kernel,
-        grid=(n // group,),
-        in_specs=[
-            pl.BlockSpec((group, cross, share), lambda i: (i, 0, 0)),
-            pl.BlockSpec((2 * cross, cross), lambda i: (0, 0)),
-        ],
-        out_specs=pl.BlockSpec((cross, group * share), lambda i: (0, i)),
-        out_shape=jax.ShapeDtypeStruct((cross, n * share), HALF),
+        in_specs=[vmem, vmem],
+        out_specs=pl.BlockSpec(memory_space=pltpu.HBM),
+        out_shape=pltpu.HBM((cross, n * share), HALF),
+        scratch_shapes=[
+            pltpu.VMEM((cross, n * share), HALF),
+            pltpu.SemaphoreType.DMA((n // group,)),
+        ],
         compiler_params=pltpu.CompilerParams(vmem_limit_bytes=VMEM_LIMIT),
         name="left_products",
     )(in_vmem(sorted_x), in_vmem(k_left))
@@ -393,7 +418,6 @@
     near = [1 << i for i in range(3)]
     far = [1 << i for i in range(3, n.bit_length() - 1)]
     packed, x = packed_grams(p_left, w_cols, phi_right, v_cols, residual)
-    packed = split(packed, near[0])
     mine = sort_by_owner(x, n)
     for reach in far[:-1]:
         packed = packed + swap(packed, reach)
@@ -401,10 +425,10 @@
     other = swap(packed, far[-1])
     owned = lax.all_to_all(mine, "rows", split_axis=0, concat_axis=0, tiled=True)
     packed = packed + other
+    packed = split(packed, near[0])
     for reach in near[1:]:
-        packed = split(packed, reach)
-    for reach in reversed(near):
-        packed = join(packed, reach)
+        packed = packed + swap(packed, reach)
+    packed = join(packed, near[0])
     k_left, k_right, u, rms = small_algebra(packed, rank, cols, float(local * n))
     update, q_right = right_products(p_left, w_cols, phi_right, v_cols, k_right, u)
     q_left = left_products(owned, k_left)

time: 119 us -> 113 us (0.950)
  starting transfers between devices: 16.9 us -> 14.2 us
  waiting for transfers between devices: 72.2 us -> 69.8 us
    ppermute x8 -> x6, starting transfers between devices: 12 us -> 8.92 us  [swap(): return lax.ppermute(x, 'rows', [(i, i ^ reach) for i in range(n)])]
    ppermute x8 -> x6, waiting for transfers between devices: 72.2 us -> 69.8 us  [swap(): return lax.ppermute(x, 'rows', [(i, i ^ reach) for i in range(n)])]
  transfers between devices with their start and end apart: 9 -> 7, of which waited for: 7 -> 5; matrix products, arithmetic and copies ran while one was open for 0% -> 1% of each run, Pallas kernels for 18% -> 19%
where the time goes in v2:
time: 113 us
  waiting for transfers between devices  69.8 us (62%)
  Pallas kernels  27.3 us (24%)
  starting transfers between devices  14.2 us (13%)
    ppermute x6, waiting for transfers between devices, swap(): return lax.ppermute(x, 'rows', [(i, i ^ reach) for i in range(n)])  69.8 us
    pallas_call x1, Pallas kernels, small_algebra(): pl.pallas_call(functools.partial(small_kernel, rank, count), in_specs=[vm...  12.2 us
    ppermute x6, starting transfers between devices, swap(): return lax.ppermute(x, 'rows', [(i, i ^ reach) for i in range(n)])  8.92 us
    pallas_call x1, Pallas kernels, right_products(): pl.pallas_call(right_kernel, grid=(local // wide,), in_specs=[spec(rank),...  5.46 us
    all_to_all x1, starting transfers between devices, shards(): lax.all_to_all(mine, 'rows', split_axis=0, concat_axis=0, tiled=True)  5.32 us
    pallas_call x1, Pallas kernels, packed_grams(): pl.pallas_call(functools.partial(gram_kernel, chunks), in_specs=[hbm] * 5...  3.66 us
    pallas_call x1, Pallas kernels, sort_by_owner(): pl.pallas_call(functools.partial(sort_kernel, n), in_specs=[pl.BlockSpec(...  3.65 us
    pallas_call x1, Pallas kernels, left_products(): pl.pallas_call(left_kernel, in_specs=[vmem, vmem], out_specs=pl.BlockSpec...  2.33 us
  transfers between devices with their start and end apart: 7, of which 5 were waited for; matrix products, arithmetic and copies ran while one was open for 1% of the time, Pallas kernels for 19%

profile of v2, /device:TPU:0, one launch (start us, length us, event | category | flops | bytes accessed | tf_op | source)
XLA Modules:
  0.0 112.7 jit_solution(2597774153008660061)
XLA Ops:
  0.6 3.7 %packed_grams.1 = (f32[208,128]{1,0:T(8,128)S(1)}, bf16[160,8192]{1,0:T(8,128)(2,1)S(1)}) custom-call(bf16[120,8192]{1,0:T(8,128)(2,1)} %p_ref.1, bf16[40,8192]{1,0:T(8,128)(2,1)} %w_ref.1, bf16[120,8192]{1,0:T(8,128)(2,1)} %phi_ref.1, bf16[40,8192]{1,0:T(8,128)(2,1)} %v_ref.1, bf16[8192]{0:T(1024)(128)(2,1)} %res_hbm.1), custom_call_target="tpu_custom_call" | custom-call | tf_op jit(solution)/shard_map/packed_grams/pallas_call | solution.py:158
  4.3 3.1 %collective-permute-start = (f32[208,128]{1,0:T(8,128)S(1)}, f32[208,128]{1,0:T(8,128)S(1)}, u32[]{:S(2)}, u32[]{:S(2)}) collective-permute-start(f32[208,128]{1,0:T(8,128)S(1)} %get-tuple-element.15), channel_id=1, source_target_pairs={{0,8},{1,9},{2,10},{3,11},{4,12},{5,13},{6,14},{7,15},{8,0},{9,1},... | collective-permute-start | bytes 319496 | tf_op jit(solution)/shard_map/ppermute | solution.py:397
  7.4 3.6 %sort_by_owner.1 = bf16[32,160,256]{2,1,0:T(8,128)(2,1)} custom-call(bf16[160,8192]{1,0:T(8,128)(2,1)S(1)} %get-tuple-element.14.x_ref), custom_call_target="tpu_custom_call" | custom-call | tf_op jit(solution)/shard_map/sort_by_owner/pallas_call | solution.py:72
  11.1 0.0 collective-permute-done
  11.1 5.3 %all-to-all-start = ((bf16[32,160,256]{2,1,0:T(8,128)(2,1)}), bf16[32,160,256]{2,1,0:T(8,128)(2,1)S(1)}, u32[]{:S(2)}, u32[]{:S(2)}) async-start(bf16[32,160,256]{2,1,0:T(8,128)(2,1)} %sort_by_owner.1), calls=%async_computation | async-start | bytes 5242880 | tf_op jit(solution)/shard_map/all_to_all | solution.py:426
  16.4 2.7 %collective-permute-start.1 = (f32[208,128]{1,0:T(8,128)S(1)}, f32[208,128]{1,0:T(8,128)S(1)}, u32[]{:S(2)}, u32[]{:S(2)}) collective-permute-start(f32[208,128]{1,0:T(8,128)S(1)} %add.21), channel_id=1, source_target_pairs={{0,16},{1,17},{2,18},{3,19},{4,20},{5,21},{6,22},{7,23},{8,24},{9,... | collective-permute-start | bytes 319496 | tf_op jit(solution)/shard_map/ppermute | solution.py:397
  19.2 61.9 %collective-permute-done.1 = f32[208,128]{1,0:T(8,128)S(1)} collective-permute-done((f32[208,128]{1,0:T(8,128)S(1)}, f32[208,128]{1,0:T(8,128)S(1)}, u32[]{:S(2)}, u32[]{:S(2)}) %collective-permute-start.1) | collective-permute-done | bytes 106528 | tf_op jit(solution)/shard_map/ppermute | solution.py:397
  81.1 0.1 collective-permute-start.2
  81.2 1.2 %collective-permute-done.2 = f32[104,128]{1,0:T(8,128)S(1)} collective-permute-done((f32[104,128]{1,0:T(8,128)S(1)}, f32[104,128]{1,0:T(8,128)S(1)}, u32[]{:S(2)}, u32[]{:S(2)}) %collective-permute-start.2) | collective-permute-done | bytes 53280 | tf_op jit(solution)/shard_map/ppermute | solution.py:397
  82.4 1.5 %collective-permute-start.3 = (f32[104,128]{1,0:T(8,128)S(1)}, f32[104,128]{1,0:T(8,128)S(1)}, u32[]{:S(2)}, u32[]{:S(2)}) collective-permute-start(f32[104,128]{1,0:T(8,128)S(1)} %dynamic-slice_add_fusion), channel_id=1, source_target_pairs={{0,2},{1,3},{2,0},{3,1},{4,6},{5,7},{6,4},{7,5},{8,10},{9,11},{10,... | collective-permute-start | bytes 159752 | tf_op jit(solution)/shard_map/ppermute | solution.py:397
  83.9 2.7 %collective-permute-done.3 = f32[104,128]{1,0:T(8,128)S(1)} collective-permute-done((f32[104,128]{1,0:T(8,128)S(1)}, f32[104,128]{1,0:T(8,128)S(1)}, u32[]{:S(2)}, u32[]{:S(2)}) %collective-permute-start.3) | collective-permute-done | bytes 53280 | tf_op jit(solution)/shard_map/ppermute | solution.py:397
  86.6 1.4 %collective-permute-start.4 = (f32[104,128]{1,0:T(8,128)S(1)}, f32[104,128]{1,0:T(8,128)S(1)}, u32[]{:S(2)}, u32[]{:S(2)}) collective-permute-start(f32[104,128]{1,0:T(8,128)S(1)} %add.26), channel_id=1, source_target_pairs={{0,4},{1,5},{2,6},{3,7},{4,0},{5,1},{6,2},{7,3},{8,12},{9,13},{10,... | collective-permute-start | bytes 159752 | tf_op jit(solution)/shard_map/ppermute | solution.py:397
  88.0 2.8 %collective-permute-done.4 = f32[104,128]{1,0:T(8,128)S(1)} collective-permute-done((f32[104,128]{1,0:T(8,128)S(1)}, f32[104,128]{1,0:T(8,128)S(1)}, u32[]{:S(2)}, u32[]{:S(2)}) %collective-permute-start.4) | collective-permute-done | bytes 53280 | tf_op jit(solution)/shard_map/ppermute | solution.py:397
  90.8 0.1 collective-permute-start.5
  90.9 1.2 %collective-permute-done.5 = f32[104,128]{1,0:T(8,128)S(1)} collective-permute-done((f32[104,128]{1,0:T(8,128)S(1)}, f32[104,128]{1,0:T(8,128)S(1)}, u32[]{:S(2)}, u32[]{:S(2)}) %collective-permute-start.5) | collective-permute-done | bytes 53280 | tf_op jit(solution)/shard_map/ppermute | solution.py:397
  92.2 12.2 %small_algebra.1 = (bf16[320,160]{1,0:T(8,128)(2,1)S(1)}, bf16[320,160]{1,0:T(8,128)(2,1)S(1)}, f32[8,160]{1,0:T(8,128)S(1)}, f32[1,128]{1,0:T(1,128)S(1)}) custom-call(f32[208,128]{1,0:T(8,128)S(1)} %maximum_select_fusion.g_ref), custom_call_target="tpu_custom_call" | custom-call | tf_op jit(solution)/shard_map/small_algebra/pallas_call | solution.py:303
  104.4 5.5 %right_products.1 = (f32[1,8192]{1,0:T(1,128)}, bf16[160,8192]{1,0:T(8,128)(2,1)}) custom-call(bf16[120,8192]{1,0:T(8,128)(2,1)} %p_ref.1, bf16[40,8192]{1,0:T(8,128)(2,1)} %w_ref.1, bf16[120,8192]{1,0:T(8,128)(2,1)} %phi_ref.1, bf16[40,8192]{1,0:T(8,128)(2,1)} %v_ref.1, bf16[320,160]{1,0:T(8,128)(2,1)S(1)} %get-tuple-element.17.k_ref, ...), custom_call_target="tpu_custom_call" | custom-call | tf_op jit(solution)/shard_map/right_products/pallas_call | solution.py:340
  109.8 0.5 slice_bitcast_fusion
  110.3 0.0 all-to-all-done.x_ref
  110.3 2.3 %left_products.1 = bf16[160,8192]{1,0:T(8,128)(2,1)} custom-call(bf16[32,160,256]{2,1,0:T(8,128)(2,1)S(1)} %all-to-all-done.x_ref, bf16[320,160]{1,0:T(8,128)(2,1)S(1)} %get-tuple-element.21.k_ref), custom_call_target="tpu_custom_call" | custom-call | tf_op jit(solution)/shard_map/left_products/pallas_call | solution.py:381
  (7 shorter events, 0.1 us)
Async XLA Ops:
  4.3 6.8 %collective-permute-start = (f32[208,128]{1,0:T(8,128)S(1)}, f32[208,128]{1,0:T(8,128)S(1)}, u32[]{:S(2)}, u32[]{:S(2)}) collective-permute-start(f32[208,128]{1,0:T(8,128)S(1)} %get-tuple-element.15), channel_id=1, source_target_pairs={{0,8},{1,9},{2,10},{3,11},{4,12},{5,13},{6,14},{7,15},{8,0},{9,1},... | collective-permute-start | bytes 319496 | tf_op jit(solution)/shard_map/ppermute | solution.py:397
  11.1 99.2 %all-to-all-start = ((bf16[32,160,256]{2,1,0:T(8,128)(2,1)}), bf16[32,160,256]{2,1,0:T(8,128)(2,1)S(1)}, u32[]{:S(2)}, u32[]{:S(2)}) async-start(bf16[32,160,256]{2,1,0:T(8,128)(2,1)} %sort_by_owner.1), calls=%async_computation | async-start | bytes 5242880 | tf_op jit(solution)/shard_map/all_to_all | solution.py:426
  16.4 64.6 %collective-permute-start.1 = (f32[208,128]{1,0:T(8,128)S(1)}, f32[208,128]{1,0:T(8,128)S(1)}, u32[]{:S(2)}, u32[]{:S(2)}) collective-permute-start(f32[208,128]{1,0:T(8,128)S(1)} %add.21), channel_id=1, source_target_pairs={{0,16},{1,17},{2,18},{3,19},{4,20},{5,21},{6,22},{7,23},{8,24},{9,... | collective-permute-start | bytes 319496 | tf_op jit(solution)/shard_map/ppermute | solution.py:397
  81.1 1.3 %collective-permute-start.2 = (f32[104,128]{1,0:T(8,128)S(1)}, f32[104,128]{1,0:T(8,128)S(1)}, u32[]{:S(2)}, u32[]{:S(2)}) collective-permute-start(f32[104,128]{1,0:T(8,128)S(1)} %constant_dynamic-slice_fusion), channel_id=1, source_target_pairs={{0,1},{1,0},{2,3},{3,2},{4,5},{5,4},{6,7},{7,6},{8,9},{9,8},{10,11... | collective-permute-start | bytes 159752 | tf_op jit(solution)/shard_map/ppermute | solution.py:397
  82.4 4.2 %collective-permute-start.3 = (f32[104,128]{1,0:T(8,128)S(1)}, f32[104,128]{1,0:T(8,128)S(1)}, u32[]{:S(2)}, u32[]{:S(2)}) collective-permute-start(f32[104,128]{1,0:T(8,128)S(1)} %dynamic-slice_add_fusion), channel_id=1, source_target_pairs={{0,2},{1,3},{2,0},{3,1},{4,6},{5,7},{6,4},{7,5},{8,10},{9,11},{10,... | collective-permute-start | bytes 159752 | tf_op jit(solution)/shard_map/ppermute | solution.py:397
  86.6 4.2 %collective-permute-start.4 = (f32[104,128]{1,0:T(8,128)S(1)}, f32[104,128]{1,0:T(8,128)S(1)}, u32[]{:S(2)}, u32[]{:S(2)}) collective-permute-start(f32[104,128]{1,0:T(8,128)S(1)} %add.26), channel_id=1, source_target_pairs={{0,4},{1,5},{2,6},{3,7},{4,0},{5,1},{6,2},{7,3},{8,12},{9,13},{10,... | collective-permute-start | bytes 159752 | tf_op jit(solution)/shard_map/ppermute | solution.py:397
  90.8 1.3 %collective-permute-start.5 = (f32[104,128]{1,0:T(8,128)S(1)}, f32[104,128]{1,0:T(8,128)S(1)}, u32[]{:S(2)}, u32[]{:S(2)}) collective-permute-start(f32[104,128]{1,0:T(8,128)S(1)} %add.27), channel_id=1, source_target_pairs={{0,1},{1,0},{2,3},{3,2},{4,5},{5,4},{6,7},{7,6},{8,9},{9,8},{10,11... | collective-permute-start | bytes 159752 | tf_op jit(solution)/shard_map/ppermute | solution.py:397

commit v3 on v2

--- a/solution.py
+++ b/solution.py
@@ -46,7 +46,6 @@
     row, column = iota((tile, tile), 0), iota((tile, tile), 1)
     wanted = lax.rem(row, runs) * n + lax.div(row, runs)
     permutation = jnp.where(column == wanted, 1.0, 0.0).astype(HALF)
-    eye = jnp.where(iota((cross, cross), 0) == iota((cross, cross), 1), 1.0, 0.0).astype(HALF)
     pair = 16 // runs if runs < 16 else 1
     for at in range(0, local, tile * pair):
         parts = []
@@ -58,10 +57,11 @@
         turned[:, rows, :] = jnp.concatenate(parts, 1).astype(HALF)
     copies = []
     for owner in range(n):
-        mine = lax.dot_general(eye, turned[owner], NT, preferred_element_type=SINGLE)
-        ready[owner] = mine.astype(HALF)
+        ready[owner] = turned[owner].T
         copies.append(pltpu.make_async_copy(ready.at[owner], out_ref.at[owner], sem.at[owner]))
-        copies[-1].start()
+        if owner:
+            copies[-2].start()
+    copies[-1].start()
     for copy in copies:
         copy.wait()
 
@@ -223,7 +223,7 @@
         ref[pl.ds(pl.multiple_of(k - top, BLOCK), BLOCK), :] = done
 
 
-def small_kernel(rank, count, g_ref, kl_ref, kr_ref, u_ref, rms_ref, left, right, tail):
+def small_kernel(rank, count, g_ref, top_ref, low_ref, kr_ref, u_ref, rms_ref, left, right, tail):
     cross = left.shape[0]
     m = LANES
     e = cross - m
@@ -290,11 +290,17 @@
     lax.fori_loop(
         0, cross // BLOCK, lambda b, c: (eliminate([left, right], [0, 0], b * BLOCK), c)[1], 0
     )
-    for source, turn, out in ((left, t_left, kl_ref), (right, t_right, kr_ref)):
-        k = dot_hi(source[...], turn)
-        k0 = to_half(k)
-        out[0:cross, :] = k0.astype(HALF)
-        out[cross : 2 * cross, :] = (k - k0).astype(HALF)
+    k = dot_hi(left[...], t_left)
+    k0 = to_half(k)
+    k1 = k - k0
+    top_ref[:, 0:m] = k0[0:m, 0:m].astype(HALF)
+    top_ref[:, m : 2 * m] = k1[0:m, 0:m].astype(HALF)
+    low_ref[0:e, :] = k0[m:cross, :].astype(HALF)
+    low_ref[e : 2 * e, :] = k1[m:cross, :].astype(HALF)
+    k = dot_hi(right[...], t_right)
+    k0 = to_half(k)
+    kr_ref[0:cross, :] = k0.astype(HALF)
+    kr_ref[cross : 2 * cross, :] = (k - k0).astype(HALF)
 
 
 def small_algebra(packed, rank, cols, count):
@@ -303,9 +309,10 @@
     return pl.pallas_call(
         functools.partial(small_kernel, rank, count),
         in_specs=[vmem],
-        out_specs=[vmem] * 4,
+        out_specs=[vmem] * 5,
         out_shape=[
-            pltpu.VMEM((2 * cross, cross), HALF),
+            pltpu.VMEM((LANES, 2 * LANES), HALF),
+            pltpu.VMEM((2 * (cross - LANES), cross), HALF),
             pltpu.VMEM((2 * cross, cross), HALF),
             pltpu.VMEM((BLOCK, cross), SINGLE),
             jax.ShapeDtypeStruct((1, LANES), SINGLE),
@@ -355,32 +362,37 @@
     )(*in_hbm(p_left, w_cols, phi_right, v_cols), in_vmem(k_right), in_vmem(u))
 
 
-def left_kernel(x_ref, k_ref, q_ref, ready, sem):
+def left_kernel(x_ref, top_ref, low_ref, q_ref, ready, sem):
     n, cross, share = x_ref.shape
+    m = LANES
+    e = cross - m
     group = n // sem.shape[0]
     wide = group * share
-    k = k_ref[...]
     copies = []
     for at in range(sem.shape[0]):
         for i in range(group):
-            both = jnp.dot(k, x_ref[at * group + i], preferred_element_type=SINGLE)
-            ready[:, at * wide + i * share : at * wide + (i + 1) * share] = (
-                both[0:cross] + both[cross : 2 * cross]
-            ).astype(HALF)
+            x = x_ref[at * group + i]
+            cut = slice(at * wide + i * share, at * wide + (i + 1) * share)
+            twice = jnp.concatenate([x[0:m], x[0:m]], 0)
+            ready[0:m, cut] = jnp.dot(top_ref[...], twice, preferred_element_type=SINGLE).astype(HALF)
+            low = jnp.dot(low_ref[...], x, preferred_element_type=SINGLE)
+            ready[m:cross, cut] = (low[0:e] + low[e : 2 * e]).astype(HALF)
         cut = pl.ds(at * wide, wide)
         copies.append(pltpu.make_async_copy(ready.at[:, cut], q_ref.at[:, cut], sem.at[at]))
-        copies[-1].start()
+        if at:
+            copies[-2].start()
+    copies[-1].start()
     for copy in copies:
         copy.wait()
 
 
-def left_products(sorted_x, k_left):
+def left_products(sorted_x, top, low):
     n, cross, share = sorted_x.shape
     group = max(1, 512 // share)
     vmem = pl.BlockSpec(memory_space=pltpu.VMEM)
     return pl.pallas_call(
         left_kernel,
-        in_specs=[vmem, vmem],
+        in_specs=[vmem, vmem, vmem],
         out_specs=pl.BlockSpec(memory_space=pltpu.HBM),
         out_shape=pltpu.HBM((cross, n * share), HALF),
         scratch_shapes=[
@@ -389,7 +401,7 @@
         ],
         compiler_params=pltpu.CompilerParams(vmem_limit_bytes=VMEM_LIMIT),
         name="left_products",
-    )(in_vmem(sorted_x), in_vmem(k_left))
+    )(in_vmem(sorted_x), in_vmem(top), in_vmem(low))
 
 
 def swap(x, reach):
@@ -429,9 +441,9 @@
     for reach in near[1:]:
         packed = packed + swap(packed, reach)
     packed = join(packed, near[0])
-    k_left, k_right, u, rms = small_algebra(packed, rank, cols, float(local * n))
+    k_top, k_low, k_right, u, rms = small_algebra(packed, rank, cols, float(local * n))
     update, q_right = right_products(p_left, w_cols, phi_right, v_cols, k_right, u)
-    q_left = left_products(owned, k_left)
+    q_left = left_products(owned, k_top, k_low)
     return (update.reshape(local), q_left, q_right, rms[0, 0:2])
 
 

time: 113 us -> 113 us (level)
  transfers between devices with their start and end apart: 7 -> 7, of which waited for: 5 -> 5; matrix products, arithmetic and copies ran while one was open for 1% -> 1% of each run, Pallas kernels for 19% -> 18%
where the time goes in v3:
time: 113 us; the launch traced here: 112 us
  waiting for transfers between devices  69.8 us (62%)
  Pallas kernels  26.4 us (23%)
  starting transfers between devices  14.8 us (13%)
    ppermute x6, waiting for transfers between devices, swap(): return lax.ppermute(x, 'rows', [(i, i ^ reach) for i in range(n)])  69.8 us
    pallas_call x1, Pallas kernels, small_algebra(): pl.pallas_call(functools.partial(small_kernel, rank, count), in_specs=[vm...  12.2 us
    ppermute x6, starting transfers between devices, swap(): return lax.ppermute(x, 'rows', [(i, i ^ reach) for i in range(n)])  8.92 us
    all_to_all x1, starting transfers between devices, shards(): lax.all_to_all(mine, 'rows', split_axis=0, concat_axis=0, tiled=True)  5.93 us
    pallas_call x1, Pallas kernels, right_products(): pl.pallas_call(right_kernel, grid=(local // wide,), in_specs=[spec(rank),...  5.46 us
    pallas_call x1, Pallas kernels, packed_grams(): pl.pallas_call(functools.partial(gram_kernel, chunks), in_specs=[hbm] * 5...  3.66 us
    pallas_call x1, Pallas kernels, sort_by_owner(): pl.pallas_call(functools.partial(sort_kernel, n), in_specs=[pl.BlockSpec(...  3.04 us
  transfers between devices with their start and end apart: 7, of which 5 were waited for; matrix products, arithmetic and copies ran while one was open for 1% of the time, Pallas kernels for 18%

profile of v3, /device:TPU:0, one launch (start us, length us, event | category | flops | bytes accessed | tf_op | source)
XLA Modules:
  0.0 112.4 jit_solution(16718576523461692553)
XLA Ops:
  0.6 3.7 %packed_grams.1 = (f32[208,128]{1,0:T(8,128)S(1)}, bf16[160,8192]{1,0:T(8,128)(2,1)S(1)}) custom-call(bf16[120,8192]{1,0:T(8,128)(2,1)} %p_ref.1, bf16[40,8192]{1,0:T(8,128)(2,1)} %w_ref.1, bf16[120,8192]{1,0:T(8,128)(2,1)} %phi_ref.1, bf16[40,8192]{1,0:T(8,128)(2,1)} %v_ref.1, bf16[8192]{0:T(1024)(128)(2,1)} %res_hbm.1), custom_call_target="tpu_custom_call" | custom-call | tf_op jit(solution)/shard_map/packed_grams/pallas_call | solution.py:158
  4.3 3.1 %collective-permute-start = (f32[208,128]{1,0:T(8,128)S(1)}, f32[208,128]{1,0:T(8,128)S(1)}, u32[]{:S(2)}, u32[]{:S(2)}) collective-permute-start(f32[208,128]{1,0:T(8,128)S(1)} %get-tuple-element.16), channel_id=1, source_target_pairs={{0,8},{1,9},{2,10},{3,11},{4,12},{5,13},{6,14},{7,15},{8,0},{9,1},... | collective-permute-start | bytes 319496 | tf_op jit(solution)/shard_map/ppermute | solution.py:409
  7.4 3.0 %sort_by_owner.1 = bf16[32,160,256]{2,1,0:T(8,128)(2,1)} custom-call(bf16[160,8192]{1,0:T(8,128)(2,1)S(1)} %get-tuple-element.15.x_ref), custom_call_target="tpu_custom_call" | custom-call | tf_op jit(solution)/shard_map/sort_by_owner/pallas_call | solution.py:72
  10.5 0.0 collective-permute-done
  10.5 5.9 %all-to-all-start = ((bf16[32,160,256]{2,1,0:T(8,128)(2,1)}), bf16[32,160,256]{2,1,0:T(8,128)(2,1)S(1)}, u32[]{:S(2)}, u32[]{:S(2)}) async-start(bf16[32,160,256]{2,1,0:T(8,128)(2,1)} %sort_by_owner.1), calls=%async_computation | async-start | bytes 5242880 | tf_op jit(solution)/shard_map/all_to_all | solution.py:438
  16.4 2.7 %collective-permute-start.1 = (f32[208,128]{1,0:T(8,128)S(1)}, f32[208,128]{1,0:T(8,128)S(1)}, u32[]{:S(2)}, u32[]{:S(2)}) collective-permute-start(f32[208,128]{1,0:T(8,128)S(1)} %add.21), channel_id=1, source_target_pairs={{0,16},{1,17},{2,18},{3,19},{4,20},{5,21},{6,22},{7,23},{8,24},{9,... | collective-permute-start | bytes 319496 | tf_op jit(solution)/shard_map/ppermute | solution.py:409
  19.2 61.9 %collective-permute-done.1 = f32[208,128]{1,0:T(8,128)S(1)} collective-permute-done((f32[208,128]{1,0:T(8,128)S(1)}, f32[208,128]{1,0:T(8,128)S(1)}, u32[]{:S(2)}, u32[]{:S(2)}) %collective-permute-start.1) | collective-permute-done | bytes 106528 | tf_op jit(solution)/shard_map/ppermute | solution.py:409
  81.1 0.1 collective-permute-start.2
  81.2 1.2 %collective-permute-done.2 = f32[104,128]{1,0:T(8,128)S(1)} collective-permute-done((f32[104,128]{1,0:T(8,128)S(1)}, f32[104,128]{1,0:T(8,128)S(1)}, u32[]{:S(2)}, u32[]{:S(2)}) %collective-permute-start.2) | collective-permute-done | bytes 53280 | tf_op jit(solution)/shard_map/ppermute | solution.py:409
  82.4 1.5 %collective-permute-start.3 = (f32[104,128]{1,0:T(8,128)S(1)}, f32[104,128]{1,0:T(8,128)S(1)}, u32[]{:S(2)}, u32[]{:S(2)}) collective-permute-start(f32[104,128]{1,0:T(8,128)S(1)} %dynamic-slice_add_fusion), channel_id=1, source_target_pairs={{0,2},{1,3},{2,0},{3,1},{4,6},{5,7},{6,4},{7,5},{8,10},{9,11},{10,... | collective-permute-start | bytes 159752 | tf_op jit(solution)/shard_map/ppermute | solution.py:409
  83.9 2.7 %collective-permute-done.3 = f32[104,128]{1,0:T(8,128)S(1)} collective-permute-done((f32[104,128]{1,0:T(8,128)S(1)}, f32[104,128]{1,0:T(8,128)S(1)}, u32[]{:S(2)}, u32[]{:S(2)}) %collective-permute-start.3) | collective-permute-done | bytes 53280 | tf_op jit(solution)/shard_map/ppermute | solution.py:409
  86.6 1.4 %collective-permute-start.4 = (f32[104,128]{1,0:T(8,128)S(1)}, f32[104,128]{1,0:T(8,128)S(1)}, u32[]{:S(2)}, u32[]{:S(2)}) collective-permute-start(f32[104,128]{1,0:T(8,128)S(1)} %add.26), channel_id=1, source_target_pairs={{0,4},{1,5},{2,6},{3,7},{4,0},{5,1},{6,2},{7,3},{8,12},{9,13},{10,... | collective-permute-start | bytes 159752 | tf_op jit(solution)/shard_map/ppermute | solution.py:409
  88.0 2.8 %collective-permute-done.4 = f32[104,128]{1,0:T(8,128)S(1)} collective-permute-done((f32[104,128]{1,0:T(8,128)S(1)}, f32[104,128]{1,0:T(8,128)S(1)}, u32[]{:S(2)}, u32[]{:S(2)}) %collective-permute-start.4) | collective-permute-done | bytes 53280 | tf_op jit(solution)/shard_map/ppermute | solution.py:409
  90.8 0.1 collective-permute-start.5
  90.9 1.2 %collective-permute-done.5 = f32[104,128]{1,0:T(8,128)S(1)} collective-permute-done((f32[104,128]{1,0:T(8,128)S(1)}, f32[104,128]{1,0:T(8,128)S(1)}, u32[]{:S(2)}, u32[]{:S(2)}) %collective-permute-start.5) | collective-permute-done | bytes 53280 | tf_op jit(solution)/shard_map/ppermute | solution.py:409
  92.2 12.2 %small_algebra.1 = (bf16[128,256]{1,0:T(8,128)(2,1)S(1)}, bf16[64,160]{1,0:T(8,128)(2,1)S(1)}, bf16[320,160]{1,0:T(8,128)(2,1)S(1)}, f32[8,160]{1,0:T(8,128)S(1)}, f32[1,128]{1,0:T(1,128)S(1)}) custom-call(f32[208,128]{1,0:T(8,128)S(1)} %maximum_select_fusion.g_ref), custom_call_target="tpu_custom_call" | custom-call | tf_op jit(solution)/shard_map/small_algebra/pallas_call | solution.py:309
  104.4 5.5 %right_products.1 = (f32[1,8192]{1,0:T(1,128)}, bf16[160,8192]{1,0:T(8,128)(2,1)}) custom-call(bf16[120,8192]{1,0:T(8,128)(2,1)} %p_ref.1, bf16[40,8192]{1,0:T(8,128)(2,1)} %w_ref.1, bf16[120,8192]{1,0:T(8,128)(2,1)} %phi_ref.1, bf16[40,8192]{1,0:T(8,128)(2,1)} %v_ref.1, bf16[320,160]{1,0:T(8,128)(2,1)S(1)} %get-tuple-element.18.k_ref, ...), custom_call_target="tpu_custom_call" | custom-call | tf_op jit(solution)/shard_map/right_products/pallas_call | solution.py:347
  109.8 0.5 slice_bitcast_fusion
  110.3 0.0 all-to-all-done.x_ref
  110.3 2.1 %left_products.1 = bf16[160,8192]{1,0:T(8,128)(2,1)} custom-call(bf16[32,160,256]{2,1,0:T(8,128)(2,1)S(1)} %all-to-all-done.x_ref, bf16[128,256]{1,0:T(8,128)(2,1)S(1)} %get-tuple-element.22.top_ref, bf16[64,160]{1,0:T(8,128)(2,1)S(1)} %get-tuple-element.23.low_ref), custom_call_target="tpu_custom_call" | custom-call | tf_op jit(solution)/shard_map/left_products/pallas_call | solution.py:393
  (7 shorter events, 0.1 us)
Async XLA Ops:
  4.3 6.2 %collective-permute-start = (f32[208,128]{1,0:T(8,128)S(1)}, f32[208,128]{1,0:T(8,128)S(1)}, u32[]{:S(2)}, u32[]{:S(2)}) collective-permute-start(f32[208,128]{1,0:T(8,128)S(1)} %get-tuple-element.16), channel_id=1, source_target_pairs={{0,8},{1,9},{2,10},{3,11},{4,12},{5,13},{6,14},{7,15},{8,0},{9,1},... | collective-permute-start | bytes 319496 | tf_op jit(solution)/shard_map/ppermute | solution.py:409
  10.5 99.8 %all-to-all-start = ((bf16[32,160,256]{2,1,0:T(8,128)(2,1)}), bf16[32,160,256]{2,1,0:T(8,128)(2,1)S(1)}, u32[]{:S(2)}, u32[]{:S(2)}) async-start(bf16[32,160,256]{2,1,0:T(8,128)(2,1)} %sort_by_owner.1), calls=%async_computation | async-start | bytes 5242880 | tf_op jit(solution)/shard_map/all_to_all | solution.py:438
  16.4 64.6 %collective-permute-start.1 = (f32[208,128]{1,0:T(8,128)S(1)}, f32[208,128]{1,0:T(8,128)S(1)}, u32[]{:S(2)}, u32[]{:S(2)}) collective-permute-start(f32[208,128]{1,0:T(8,128)S(1)} %add.21), channel_id=1, source_target_pairs={{0,16},{1,17},{2,18},{3,19},{4,20},{5,21},{6,22},{7,23},{8,24},{9,... | collective-permute-start | bytes 319496 | tf_op jit(solution)/shard_map/ppermute | solution.py:409
  81.1 1.3 %collective-permute-start.2 = (f32[104,128]{1,0:T(8,128)S(1)}, f32[104,128]{1,0:T(8,128)S(1)}, u32[]{:S(2)}, u32[]{:S(2)}) collective-permute-start(f32[104,128]{1,0:T(8,128)S(1)} %constant_dynamic-slice_fusion), channel_id=1, source_target_pairs={{0,1},{1,0},{2,3},{3,2},{4,5},{5,4},{6,7},{7,6},{8,9},{9,8},{10,11... | collective-permute-start | bytes 159752 | tf_op jit(solution)/shard_map/ppermute | solution.py:409
  82.4 4.2 %collective-permute-start.3 = (f32[104,128]{1,0:T(8,128)S(1)}, f32[104,128]{1,0:T(8,128)S(1)}, u32[]{:S(2)}, u32[]{:S(2)}) collective-permute-start(f32[104,128]{1,0:T(8,128)S(1)} %dynamic-slice_add_fusion), channel_id=1, source_target_pairs={{0,2},{1,3},{2,0},{3,1},{4,6},{5,7},{6,4},{7,5},{8,10},{9,11},{10,... | collective-permute-start | bytes 159752 | tf_op jit(solution)/shard_map/ppermute | solution.py:409
  86.6 4.2 %collective-permute-start.4 = (f32[104,128]{1,0:T(8,128)S(1)}, f32[104,128]{1,0:T(8,128)S(1)}, u32[]{:S(2)}, u32[]{:S(2)}) collective-permute-start(f32[104,128]{1,0:T(8,128)S(1)} %add.26), channel_id=1, source_target_pairs={{0,4},{1,5},{2,6},{3,7},{4,0},{5,1},{6,2},{7,3},{8,12},{9,13},{10,... | collective-permute-start | bytes 159752 | tf_op jit(solution)/shard_map/ppermute | solution.py:409
  90.8 1.3 %collective-permute-start.5 = (f32[104,128]{1,0:T(8,128)S(1)}, f32[104,128]{1,0:T(8,128)S(1)}, u32[]{:S(2)}, u32[]{:S(2)}) collective-permute-start(f32[104,128]{1,0:T(8,128)S(1)} %add.27), channel_id=1, source_target_pairs={{0,1},{1,0},{2,3},{3,2},{4,5},{5,4},{6,7},{7,6},{8,9},{9,8},{10,11... | collective-permute-start | bytes 159752 | tf_op jit(solution)/shard_map/ppermute | solution.py:409

commit v4 on v3

--- a/solution.py
+++ b/solution.py
@@ -178,52 +178,70 @@
     )(*in_hbm(p_left, w_cols, phi_right, v_cols, residual))
 
 
-def eliminate(refs, tops, k):
-    panels = []
-    for ref, top in zip(refs, tops):
-        cross = ref.shape[1]
-        x = ref[pl.ds(pl.multiple_of(k - top, BLOCK), BLOCK), :]
-        lane, sub = iota((BLOCK, cross), 1), iota((BLOCK, cross), 0)
-        column = [
-            jnp.sum(jnp.where(lane == k + i, x, 0.0), 1, keepdims=True) for i in range(BLOCK)
-        ]
-        rel = lane - k
-        x = jnp.where((rel >= 0) & (rel < BLOCK), jnp.where(rel == sub, 1.0, 0.0), x)
-        panels.append([x, column, rel, sub])
+def eliminate(refs, tops):
+    crosses = [ref.shape[1] for ref in refs]
+    steps = refs[0].shape[0] // BLOCK
+    lane, sub = [iota((BLOCK, cross), 1) for cross in crosses], [iota((BLOCK, cross), 0) for cross in crosses]
     thin = iota((BLOCK, 1), 0)
-    for i in range(BLOCK):
-        for panel in panels:
-            x, column, rel, sub = panel
-            scale = lax.rsqrt(column[i][i : i + 1, :])
-            factor = jnp.where(thin > i, column[i] * scale, 0.0)
-            for j in range(i + 1, BLOCK):
-                column[j] = column[j] - factor * (column[j][i : i + 1, :] * scale)
-            row = x[i : i + 1, :] * scale
-            panel[0] = jnp.where(sub == i, row, x - factor * row)
-    for ref, top, (x, _, rel, _) in zip(refs, tops, panels):
-        cross = ref.shape[1]
-        right = jnp.where(rel >= BLOCK, x, 0.0)
-        done = jnp.where(rel < BLOCK, x, 0.0)
-        r0 = to_half(right)
-        r1 = to_half(right - r0)
-        r2 = right - r0 - r1
-        x0 = to_half(x)
-        x1 = to_half(x - x0)
-        x2 = x - x0 - x1
-        lhs = jnp.concatenate([r0, r0, r0, r1, r1, r2], 0)
-        if top:
-            lhs = jnp.concatenate([lhs, jnp.zeros((LANES - lhs.shape[0], cross), SINGLE)], 0)
+
+    def step(at, carry):
+        row_at = pl.multiple_of(at * BLOCK, BLOCK)
+        panels, befores = carry
+        for ref, top, x, lanes, cross in zip(refs, tops, befores, lane, crosses):
+            far = jnp.where(lanes - (row_at + top) >= BLOCK, x, 0.0)
+            r0 = to_half(far)
+            r1 = to_half(far - r0)
+            r2 = far - r0 - r1
+            x0 = to_half(x)
+            x1 = to_half(x - x0)
+            x2 = x - x0 - x1
+            lhs = jnp.concatenate([r0, r0, r0, r1, r1, r2] + [jnp.zeros_like(x)] * 10, 0)
             lhs = lhs.T[top:cross, 0 : 6 * BLOCK].astype(HALF)
-        else:
-            lhs = lhs.T.astype(HALF)
-        rhs = jnp.concatenate([x0, x1, x2, x0, x1, x0], 0).astype(HALF)
-        change = jnp.dot(lhs, rhs, preferred_element_type=SINGLE)
-        here = iota(ref.shape, 1) - k
-        ref[...] = jnp.where((here >= 0) & (here < BLOCK), 0.0, ref[...]) - change
-        ref[pl.ds(pl.multiple_of(k - top, BLOCK), BLOCK), :] = done
-
-
-def small_kernel(rank, count, g_ref, top_ref, low_ref, kr_ref, u_ref, rms_ref, left, right, tail):
+            rhs = jnp.concatenate([x0, x1, x2, x0, x1, x0], 0).astype(HALF)
+            change = jnp.dot(lhs, rhs, preferred_element_type=SINGLE)
+            here = iota(ref.shape, 1) - (row_at + top) + BLOCK
+            later = iota(ref.shape, 0) >= row_at + BLOCK
+            ref[...] = jnp.where((here >= 0) & (here < BLOCK) & later, 0.0, ref[...]) - change
+        columns, scaled = [], []
+        for x, top, lanes, subs in zip(panels, tops, lane, sub):
+            rel = lanes - (row_at + top)
+            columns.append([jnp.sum(jnp.where(rel == i, x, 0.0), 1, keepdims=True) for i in range(BLOCK)])
+            scaled.append(jnp.where((rel >= 0) & (rel < BLOCK), jnp.where(rel == subs, 1.0, 0.0), x))
+        for i in range(BLOCK):
+            for which, column in enumerate(columns):
+                scale = lax.rsqrt(column[i][i : i + 1, :])
+                factor = jnp.where(thin > i, column[i] * scale, 0.0)
+                for j in range(i + 1, BLOCK):
+                    column[j] = column[j] - factor * (column[j][i : i + 1, :] * scale)
+                x = scaled[which]
+                row = x[i : i + 1, :] * scale
+                scaled[which] = jnp.where(sub[which] == i, row, x - factor * row)
+        nexts = []
+        for ref, top, x, lanes, subs in zip(refs, tops, scaled, lane, sub):
+            rel = lanes - (row_at + top)
+            ref[pl.ds(row_at, BLOCK), :] = jnp.where(rel < BLOCK, x, 0.0)
+            ahead = pl.multiple_of(lax.rem(row_at + BLOCK, ref.shape[0]), BLOCK)
+            rows = jnp.where((rel >= 0) & (rel < BLOCK), 0.0, ref[pl.ds(ahead, BLOCK), :])
+            for i in range(BLOCK):
+                row = x[i : i + 1, :]
+                weight = jnp.sum(jnp.where(rel == subs + BLOCK, row, 0.0), 1, keepdims=True)
+                rows = rows - weight * row
+            nexts.append(rows)
+        return nexts, scaled
+
+    starts = [ref[0:BLOCK, :] for ref in refs]
+    lax.fori_loop(0, steps, step, (starts, [jnp.zeros_like(x) for x in starts]))
+
+
+def small_kernel(rank, count, g_ref, p_hbm, w_hbm, phi_hbm, v_hbm, *refs):
+    top_ref, low_ref, rms_ref, upd_hbm, q_hbm, left, right, tail, *buffers, update, ready, sem, out_sem = refs
+    loads = [
+        pltpu.make_async_copy(source, buffer, sem.at[i])
+        for i, (source, buffer) in enumerate(zip((p_hbm, w_hbm, phi_hbm, v_hbm), buffers))
+    ]
+    for load in loads:
+        load.start()
+
     cross = left.shape[0]
     m = LANES
     e = cross - m
@@ -256,9 +274,7 @@
     res_sq = g_ref[base + 2 : base + 3, e : e + 1]
 
     tail[...] = g_right[rank:cross, :]
-    lax.fori_loop(
-        rank // BLOCK, cross // BLOCK, lambda b, c: (eliminate([tail], [rank], b * BLOCK), c)[1], 0
-    )
+    eliminate([tail], [rank])
     low_lane = iota((cross - rank, cross), 1)
     low_row = iota((cross - rank, cross), 0)
     inverse = jnp.where(low_lane >= rank, tail[...], 0.0)
@@ -281,15 +297,13 @@
     u1 = to_half(u - u0)
     u2 = u - u0 - u1
     sub8 = iota((BLOCK, cross), 0)
-    u_ref[...] = jnp.where(sub8 == 0, u0, jnp.where(sub8 == 1, u1, jnp.where(sub8 == 2, u2, 0.0)))
+    u = jnp.where(sub8 == 0, u0, jnp.where(sub8 == 1, u1, jnp.where(sub8 == 2, u2, 0.0))).astype(HALF)
     lane_out = iota((1, LANES), 1)
     rms_ref[...] = jnp.sqrt(jnp.where(lane_out == 0, res_sq, upd_sq) / count)
 
     left[...] = dot_hi(dot_hi(t_left, g_left), t_left, NT)
     right[...] = dot_hi(dot_hi(t_right, g_right), t_right, NT)
-    lax.fori_loop(
-        0, cross // BLOCK, lambda b, c: (eliminate([left, right], [0, 0], b * BLOCK), c)[1], 0
-    )
+    eliminate([left, right], [0, 0])
     k = dot_hi(left[...], t_left)
     k0 = to_half(k)
     k1 = k - k0
@@ -297,69 +311,83 @@
     top_ref[:, m : 2 * m] = k1[0:m, 0:m].astype(HALF)
     low_ref[0:e, :] = k0[m:cross, :].astype(HALF)
     low_ref[e : 2 * e, :] = k1[m:cross, :].astype(HALF)
+
     k = dot_hi(right[...], t_right)
     k0 = to_half(k)
-    kr_ref[0:cross, :] = k0.astype(HALF)
-    kr_ref[cross : 2 * cross, :] = (k - k0).astype(HALF)
-
-
-def small_algebra(packed, rank, cols, count):
+    k1 = k - k0
+    k_top = jnp.concatenate([k0[0:m, 0:m], k1[0:m, 0:m]], 1).astype(HALF)
+    k_low = jnp.concatenate([k0[m:cross], k1[m:cross]], 0).astype(HALF)
+    for load in loads:
+        load.wait()
+    parts = out_sem.shape[0] - 1
+    wide = ready.shape[1] // parts
+    tile = 256
+
+    def piece(at):
+        cut = pl.ds(pl.multiple_of(at * wide, wide), wide)
+        return pltpu.make_async_copy(ready.at[:, cut], q_hbm.at[:, cut], out_sem.at[at])
+
+    def multiply(at, carry):
+        for to in range(0, wide, tile):
+            cut = pl.ds(pl.multiple_of(at * wide + to, tile), tile)
+            p, w, phi, v = [buffer[:, cut].astype(SINGLE) for buffer in buffers]
+            y = jnp.concatenate([phi, v], 0).astype(HALF)
+            twice = jnp.concatenate([y[0:m], y[0:m]], 0)
+            ready[0:m, cut] = jnp.dot(k_top, twice, preferred_element_type=SINGLE).astype(HALF)
+            low = jnp.dot(k_low, y, preferred_element_type=SINGLE)
+            ready[m:cross, cut] = (low[0:e] + low[e : 2 * e]).astype(HALF)
+            x = jnp.concatenate([p, w], 0).astype(HALF)
+            update[:, cut] = jnp.sum(jnp.dot(u, x, preferred_element_type=SINGLE), 0, keepdims=True)
+
+        @pl.when(at > 0)
+        def _():
+            piece(at - 1).start()
+
+        return carry
+
+    lax.fori_loop(0, parts, multiply, 0)
+    piece(parts - 1).start()
+    whole = pltpu.make_async_copy(update, upd_hbm, out_sem.at[parts])
+    whole.start()
+    for at in range(parts):
+        piece(at).wait()
+    whole.wait()
+
+
+def small_algebra(packed, p_left, w_cols, phi_right, v_cols, count):
+    rank, local = p_left.shape
+    cols = w_cols.shape[0]
     cross = rank + cols
+    parts = 4
     vmem = pl.BlockSpec(memory_space=pltpu.VMEM)
+    hbm = pl.BlockSpec(memory_space=pltpu.HBM)
     return pl.pallas_call(
         functools.partial(small_kernel, rank, count),
-        in_specs=[vmem],
-        out_specs=[vmem] * 5,
+        in_specs=[vmem] + [hbm] * 4,
+        out_specs=[vmem] * 3 + [hbm] * 2,
         out_shape=[
             pltpu.VMEM((LANES, 2 * LANES), HALF),
             pltpu.VMEM((2 * (cross - LANES), cross), HALF),
-            pltpu.VMEM((2 * cross, cross), HALF),
-            pltpu.VMEM((BLOCK, cross), SINGLE),
-            jax.ShapeDtypeStruct((1, LANES), SINGLE),
+            pltpu.VMEM((1, LANES), SINGLE),
+            pltpu.HBM((1, local), SINGLE),
+            pltpu.HBM((cross, local), HALF),
         ],
         scratch_shapes=[
             pltpu.VMEM((cross, cross), SINGLE),
             pltpu.VMEM((cross, cross), SINGLE),
             pltpu.VMEM((cols, cross), SINGLE),
+            pltpu.VMEM((rank, local), HALF),
+            pltpu.VMEM((cols, local), HALF),
+            pltpu.VMEM((rank, local), HALF),
+            pltpu.VMEM((cols, local), HALF),
+            pltpu.VMEM((1, local), SINGLE),
+            pltpu.VMEM((cross, local), HALF),
+            pltpu.SemaphoreType.DMA((4,)),
+            pltpu.SemaphoreType.DMA((parts + 1,)),
         ],
         compiler_params=pltpu.CompilerParams(vmem_limit_bytes=VMEM_LIMIT),
         name="small_algebra",
-    )(in_vmem(packed))
-
-
-def right_kernel(p_ref, w_ref, phi_ref, v_ref, k_ref, u_ref, upd_ref, q_ref):
-    cross = k_ref.shape[1]
-    y = jnp.concatenate([phi_ref[...].astype(SINGLE), v_ref[...].astype(SINGLE)], 0).astype(HALF)
-    both = jnp.dot(k_ref[...], y, preferred_element_type=SINGLE)
-    q_ref[...] = (both[0:cross] + both[cross : 2 * cross]).astype(HALF)
-    x = jnp.concatenate([p_ref[...].astype(SINGLE), w_ref[...].astype(SINGLE)], 0).astype(HALF)
-    upd_ref[...] = jnp.sum(
-        jnp.dot(u_ref[...].astype(HALF), x, preferred_element_type=SINGLE), 0, keepdims=True
-    )
-
-
-def right_products(p_left, w_cols, phi_right, v_cols, k_right, u):
-    rank, local = p_left.shape
-    cols = w_cols.shape[0]
-    cross = rank + cols
-    wide = min(local, 2048)
-    spec = lambda rows: pl.BlockSpec((rows, wide), lambda i: (0, i))
-    return pl.pallas_call(
-        right_kernel,
-        grid=(local // wide,),
-        in_specs=[
-            spec(rank), spec(cols), spec(rank), spec(cols),
-            pl.BlockSpec((2 * cross, cross), lambda i: (0, 0)),
-            pl.BlockSpec((BLOCK, cross), lambda i: (0, 0)),
-        ],
-        out_specs=[spec(1), spec(cross)],
-        out_shape=[
-            jax.ShapeDtypeStruct((1, local), SINGLE),
-            pltpu.HBM((cross, local), HALF),
-        ],
-        compiler_params=pltpu.CompilerParams(vmem_limit_bytes=VMEM_LIMIT),
-        name="right_products",
-    )(*in_hbm(p_left, w_cols, phi_right, v_cols), in_vmem(k_right), in_vmem(u))
+    )(in_vmem(packed), *in_hbm(p_left, w_cols, phi_right, v_cols))
 
 
 def left_kernel(x_ref, top_ref, low_ref, q_ref, ready, sem):
@@ -424,25 +452,24 @@
 
 
 def shards(p_left, phi_right, v_cols, w_cols, residual):
-    rank, local = p_left.shape
-    cols = v_cols.shape[0]
+    _, local = p_left.shape
     n = lax.axis_size("rows")
     near = [1 << i for i in range(3)]
     far = [1 << i for i in range(3, n.bit_length() - 1)]
     packed, x = packed_grams(p_left, w_cols, phi_right, v_cols, residual)
     mine = sort_by_owner(x, n)
-    for reach in far[:-1]:
-        packed = packed + swap(packed, reach)
-    mine, packed = lax.optimization_barrier((mine, packed))
     other = swap(packed, far[-1])
     owned = lax.all_to_all(mine, "rows", split_axis=0, concat_axis=0, tiled=True)
     packed = packed + other
     packed = split(packed, near[0])
     for reach in near[1:]:
         packed = packed + swap(packed, reach)
+    for reach in far[:-1]:
+        packed = packed + swap(packed, reach)
     packed = join(packed, near[0])
-    k_top, k_low, k_right, u, rms = small_algebra(packed, rank, cols, float(local * n))
-    update, q_right = right_products(p_left, w_cols, phi_right, v_cols, k_right, u)
+    k_top, k_low, rms, update, q_right = small_algebra(
+        packed, p_left, w_cols, phi_right, v_cols, float(local * n)
+    )
     q_left = left_products(owned, k_top, k_low)
     return (update.reshape(local), q_left, q_right, rms[0, 0:2])
 

time: 113 us -> 111 us (0.982)
  Pallas kernels: 26.4 us -> 22 us
  waiting for transfers between devices: 69.8 us -> 73.9 us
  starting transfers between devices: 14.8 us -> 13.2 us
    pallas_call x1 -> x0, Pallas kernels: 5.46 us -> none  [right_products(): pl.pallas_call(right_kernel, grid=(local // wide,), in_specs=[spec(rank),...]
    ppermute x6, waiting for transfers between devices: 69.8 us -> 73.9 us  [swap(): return lax.ppermute(x, 'rows', [(i, i ^ reach) for i in range(n)])]
    ppermute x6, starting transfers between devices: 8.92 us -> 5.87 us  [swap(): return lax.ppermute(x, 'rows', [(i, i ^ reach) for i in range(n)])]
    all_to_all x1, starting transfers between devices: 5.93 us -> 7.33 us  [shards(): lax.all_to_all(mine, 'rows', split_axis=0, concat_axis=0, tiled=True)]
  transfers between devices with their start and end apart: 7 -> 7, of which waited for: 5 -> 6; matrix products, arithmetic and copies ran while one was open for 1% -> 1% of each run, Pallas kernels for 18% -> 12%
where the time goes in v4:
time: 111 us; the launch traced here: 110 us
  waiting for transfers between devices  73.9 us (67%)
  Pallas kernels  22 us (20%)
  starting transfers between devices  13.2 us (12%)
    ppermute x6, waiting for transfers between devices, swap(): return lax.ppermute(x, 'rows', [(i, i ^ reach) for i in range(n)])  73.9 us
    pallas_call x1, Pallas kernels, small_algebra(): pl.pallas_call(functools.partial(small_kernel, rank, count), in_specs=[vm...  13.2 us
    all_to_all x1, starting transfers between devices, shards(): lax.all_to_all(mine, 'rows', split_axis=0, concat_axis=0, tiled=True)  7.33 us
    ppermute x6, starting transfers between devices, swap(): return lax.ppermute(x, 'rows', [(i, i ^ reach) for i in range(n)])  5.87 us
    pallas_call x1, Pallas kernels, packed_grams(): pl.pallas_call(functools.partial(gram_kernel, chunks), in_specs=[hbm] * 5...  3.66 us
    pallas_call x1, Pallas kernels, sort_by_owner(): pl.pallas_call(functools.partial(sort_kernel, n), in_specs=[pl.BlockSpec(...  3.04 us
  transfers between devices with their start and end apart: 7, of which 6 were waited for; matrix products, arithmetic and copies ran while one was open for 1% of the time, Pallas kernels for 12%

profile of v4, /device:TPU:0, one launch (start us, length us, event | category | flops | bytes accessed | tf_op | source)
XLA Modules:
  0.0 110.4 jit_solution(17817708594046614836)
XLA Ops:
  0.6 3.7 %packed_grams.1 = (f32[208,128]{1,0:T(8,128)S(1)}, bf16[160,8192]{1,0:T(8,128)(2,1)S(1)}) custom-call(bf16[120,8192]{1,0:T(8,128)(2,1)} %p_hbm.3, bf16[40,8192]{1,0:T(8,128)(2,1)} %w_hbm.3, bf16[120,8192]{1,0:T(8,128)(2,1)} %phi_hbm.3, bf16[40,8192]{1,0:T(8,128)(2,1)} %v_hbm.3, bf16[8192]{0:T(1024)(128)(2,1)} %res_hbm.1), custom_call_target="tpu_custom_call" | custom-call | tf_op jit(solution)/shard_map/packed_grams/pallas_call | solution.py:158
  4.3 3.0 %sort_by_owner.1 = bf16[32,160,256]{2,1,0:T(8,128)(2,1)} custom-call(bf16[160,8192]{1,0:T(8,128)(2,1)S(1)} %get-tuple-element.13.x_ref), custom_call_target="tpu_custom_call" | custom-call | tf_op jit(solution)/shard_map/sort_by_owner/pallas_call | solution.py:72
  7.4 7.3 %all-to-all-start = ((bf16[32,160,256]{2,1,0:T(8,128)(2,1)}), bf16[32,160,256]{2,1,0:T(8,128)(2,1)S(1)}, u32[]{:S(2)}, u32[]{:S(2)}) async-start(bf16[32,160,256]{2,1,0:T(8,128)(2,1)} %sort_by_owner.1), calls=%async_computation | async-start | bytes 5242880 | tf_op jit(solution)/shard_map/all_to_all | solution.py:462
  14.7 2.7 %collective-permute-start = (f32[208,128]{1,0:T(8,128)S(1)}, f32[208,128]{1,0:T(8,128)S(1)}, u32[]{:S(2)}, u32[]{:S(2)}) collective-permute-start(f32[208,128]{1,0:T(8,128)S(1)} %get-tuple-element.11), channel_id=1, source_target_pairs={{0,16},{1,17},{2,18},{3,19},{4,20},{5,21},{6,22},{7,23},{8,24},{9,... | collective-permute-start | bytes 319496 | tf_op jit(solution)/shard_map/ppermute | solution.py:437
  17.4 61.9 %collective-permute-done = f32[208,128]{1,0:T(8,128)S(1)} collective-permute-done((f32[208,128]{1,0:T(8,128)S(1)}, f32[208,128]{1,0:T(8,128)S(1)}, u32[]{:S(2)}, u32[]{:S(2)}) %collective-permute-start) | collective-permute-done | bytes 106528 | tf_op jit(solution)/shard_map/ppermute | solution.py:437
  79.4 0.1 collective-permute-start.1
  79.4 1.2 %collective-permute-done.1 = f32[104,128]{1,0:T(8,128)S(1)} collective-permute-done((f32[104,128]{1,0:T(8,128)S(1)}, f32[104,128]{1,0:T(8,128)S(1)}, u32[]{:S(2)}, u32[]{:S(2)}) %collective-permute-start.1) | collective-permute-done | bytes 53280 | tf_op jit(solution)/shard_map/ppermute | solution.py:437
  80.7 1.5 %collective-permute-start.2 = (f32[104,128]{1,0:T(8,128)S(1)}, f32[104,128]{1,0:T(8,128)S(1)}, u32[]{:S(2)}, u32[]{:S(2)}) collective-permute-start(f32[104,128]{1,0:T(8,128)S(1)} %dynamic-slice_add_fusion), channel_id=1, source_target_pairs={{0,2},{1,3},{2,0},{3,1},{4,6},{5,7},{6,4},{7,5},{8,10},{9,11},{10,... | collective-permute-start | bytes 159752 | tf_op jit(solution)/shard_map/ppermute | solution.py:437
  82.2 2.7 %collective-permute-done.2 = f32[104,128]{1,0:T(8,128)S(1)} collective-permute-done((f32[104,128]{1,0:T(8,128)S(1)}, f32[104,128]{1,0:T(8,128)S(1)}, u32[]{:S(2)}, u32[]{:S(2)}) %collective-permute-start.2) | collective-permute-done | bytes 53280 | tf_op jit(solution)/shard_map/ppermute | solution.py:437
  84.9 1.4 %collective-permute-start.3 = (f32[104,128]{1,0:T(8,128)S(1)}, f32[104,128]{1,0:T(8,128)S(1)}, u32[]{:S(2)}, u32[]{:S(2)}) collective-permute-start(f32[104,128]{1,0:T(8,128)S(1)} %add.25), channel_id=1, source_target_pairs={{0,4},{1,5},{2,6},{3,7},{4,0},{5,1},{6,2},{7,3},{8,12},{9,13},{10,... | collective-permute-start | bytes 159752 | tf_op jit(solution)/shard_map/ppermute | solution.py:437
  86.3 2.8 %collective-permute-done.3 = f32[104,128]{1,0:T(8,128)S(1)} collective-permute-done((f32[104,128]{1,0:T(8,128)S(1)}, f32[104,128]{1,0:T(8,128)S(1)}, u32[]{:S(2)}, u32[]{:S(2)}) %collective-permute-start.3) | collective-permute-done | bytes 53280 | tf_op jit(solution)/shard_map/ppermute | solution.py:437
  89.1 0.1 collective-permute-start.4
  89.2 4.1 %collective-permute-done.4 = f32[104,128]{1,0:T(8,128)S(1)} collective-permute-done((f32[104,128]{1,0:T(8,128)S(1)}, f32[104,128]{1,0:T(8,128)S(1)}, u32[]{:S(2)}, u32[]{:S(2)}) %collective-permute-start.4) | collective-permute-done | bytes 53280 | tf_op jit(solution)/shard_map/ppermute | solution.py:437
  93.3 0.1 collective-permute-start.5
  93.4 1.2 %collective-permute-done.5 = f32[104,128]{1,0:T(8,128)S(1)} collective-permute-done((f32[104,128]{1,0:T(8,128)S(1)}, f32[104,128]{1,0:T(8,128)S(1)}, u32[]{:S(2)}, u32[]{:S(2)}) %collective-permute-start.5) | collective-permute-done | bytes 53280 | tf_op jit(solution)/shard_map/ppermute | solution.py:437
  94.6 13.2 %small_algebra.1 = (bf16[128,256]{1,0:T(8,128)(2,1)S(1)}, bf16[64,160]{1,0:T(8,128)(2,1)S(1)}, f32[1,128]{1,0:T(1,128)S(1)}, f32[1,8192]{1,0:T(1,128)}, bf16[160,8192]{1,0:T(8,128)(2,1)}) custom-call(f32[208,128]{1,0:T(8,128)S(1)} %maximum_select_fusion.g_ref, bf16[120,8192]{1,0:T(8,128)(2,1)} %p_hbm.3, bf16[40,8192]{1,0:T(8,128)(2,1)} %w_hbm.3, ...), custom_call_target="tpu_custom_call" | custom-call | tf_op jit(solution)/shard_map/small_algebra/pallas_call | solution.py:364
  107.8 0.5 slice_bitcast_fusion
  108.3 0.0 all-to-all-done.x_ref
  108.4 2.1 %left_products.1 = bf16[160,8192]{1,0:T(8,128)(2,1)} custom-call(bf16[32,160,256]{2,1,0:T(8,128)(2,1)S(1)} %all-to-all-done.x_ref, bf16[128,256]{1,0:T(8,128)(2,1)S(1)} %get-tuple-element.14.top_ref, bf16[64,160]{1,0:T(8,128)(2,1)S(1)} %get-tuple-element.15.low_ref), custom_call_target="tpu_custom_call" | custom-call | tf_op jit(solution)/shard_map/left_products/pallas_call | solution.py:421
  (7 shorter events, 0.1 us)
Async XLA Ops:
  7.4 101.0 %all-to-all-start = ((bf16[32,160,256]{2,1,0:T(8,128)(2,1)}), bf16[32,160,256]{2,1,0:T(8,128)(2,1)S(1)}, u32[]{:S(2)}, u32[]{:S(2)}) async-start(bf16[32,160,256]{2,1,0:T(8,128)(2,1)} %sort_by_owner.1), calls=%async_computation | async-start | bytes 5242880 | tf_op jit(solution)/shard_map/all_to_all | solution.py:462
  14.7 64.6 %collective-permute-start = (f32[208,128]{1,0:T(8,128)S(1)}, f32[208,128]{1,0:T(8,128)S(1)}, u32[]{:S(2)}, u32[]{:S(2)}) collective-permute-start(f32[208,128]{1,0:T(8,128)S(1)} %get-tuple-element.11), channel_id=1, source_target_pairs={{0,16},{1,17},{2,18},{3,19},{4,20},{5,21},{6,22},{7,23},{8,24},{9,... | collective-permute-start | bytes 319496 | tf_op jit(solution)/shard_map/ppermute | solution.py:437
  79.4 1.3 %collective-permute-start.1 = (f32[104,128]{1,0:T(8,128)S(1)}, f32[104,128]{1,0:T(8,128)S(1)}, u32[]{:S(2)}, u32[]{:S(2)}) collective-permute-start(f32[104,128]{1,0:T(8,128)S(1)} %constant_dynamic-slice_fusion), channel_id=1, source_target_pairs={{0,1},{1,0},{2,3},{3,2},{4,5},{5,4},{6,7},{7,6},{8,9},{9,8},{10,11... | collective-permute-start | bytes 159752 | tf_op jit(solution)/shard_map/ppermute | solution.py:437
  80.7 4.2 %collective-permute-start.2 = (f32[104,128]{1,0:T(8,128)S(1)}, f32[104,128]{1,0:T(8,128)S(1)}, u32[]{:S(2)}, u32[]{:S(2)}) collective-permute-start(f32[104,128]{1,0:T(8,128)S(1)} %dynamic-slice_add_fusion), channel_id=1, source_target_pairs={{0,2},{1,3},{2,0},{3,1},{4,6},{5,7},{6,4},{7,5},{8,10},{9,11},{10,... | collective-permute-start | bytes 159752 | tf_op jit(solution)/shard_map/ppermute | solution.py:437
  84.9 4.2 %collective-permute-start.3 = (f32[104,128]{1,0:T(8,128)S(1)}, f32[104,128]{1,0:T(8,128)S(1)}, u32[]{:S(2)}, u32[]{:S(2)}) collective-permute-start(f32[104,128]{1,0:T(8,128)S(1)} %add.25), channel_id=1, source_target_pairs={{0,4},{1,5},{2,6},{3,7},{4,0},{5,1},{6,2},{7,3},{8,12},{9,13},{10,... | collective-permute-start | bytes 159752 | tf_op jit(solution)/shard_map/ppermute | solution.py:437
  89.1 4.2 %collective-permute-start.4 = (f32[104,128]{1,0:T(8,128)S(1)}, f32[104,128]{1,0:T(8,128)S(1)}, u32[]{:S(2)}, u32[]{:S(2)}) collective-permute-start(f32[104,128]{1,0:T(8,128)S(1)} %add.26), channel_id=1, source_target_pairs={{0,8},{1,9},{2,10},{3,11},{4,12},{5,13},{6,14},{7,15},{8,0},{9,1},... | collective-permute-start | bytes 159752 | tf_op jit(solution)/shard_map/ppermute | solution.py:437
  93.3 1.3 %collective-permute-start.5 = (f32[104,128]{1,0:T(8,128)S(1)}, f32[104,128]{1,0:T(8,128)S(1)}, u32[]{:S(2)}, u32[]{:S(2)}) collective-permute-start(f32[104,128]{1,0:T(8,128)S(1)} %add.27), channel_id=1, source_target_pairs={{0,1},{1,0},{2,3},{3,2},{4,5},{5,4},{6,7},{7,6},{8,9},{9,8},{10,11... | collective-permute-start | bytes 159752 | tf_op jit(solution)/shard_map/ppermute | solution.py:437
